TPU v7x, 32 devices: a whole 2x2x4 slice. The times are simulated.
32 devices in a mesh: pool: 32 (over z, y, x, core).
Axes of the slice: x: 2, y: 2, z: 4, core: 2. Of those that a mesh axis runs over, the one named last changes fastest.
Arguments:
- hidden: bfloat16 [32, 64, 7168], P('pool')
- prefix_len: int32 [32], P('pool')
- prefix_table: int32 [32, 64, 2], P('pool')
- write_table: int32 [32, 1, 2], P('pool')
- cache_c: bfloat16 [32, 65, 64, 512], P('pool')
- cache_kr: bfloat16 [32, 65, 64, 64], P('pool')
- w_q: bfloat16 [7168, 12288], replicated
- w_dkv: bfloat16 [7168, 576], replicated
- g_kv: bfloat16 [512], replicated
- w_uk: bfloat16 [512, 64, 128], replicated
- w_uv: bfloat16 [512, 64, 128], replicated
- w_o: bfloat16 [8192, 7168], replicated
Outputs:
- output 1: bfloat16 [32, 64, 7168], P('pool')
- output 2: bfloat16 [32, 65, 64, 512], P('pool')
- output 3: bfloat16 [32, 65, 64, 64], P('pool')
All inputs are finite; a program needn't handle non-finite values.
Results may differ from a plain program's by a relative error of at most 0.00640782.
Values are sent between devices in bfloat16 or wider.
A program may use at most 1.25 GiB of HBM per device.

v0:
```python
import jax
import jax.numpy as jnp
from jax import lax
from jax.sharding import PartitionSpec as P

PAGE_LEN = 64
LATENT = 512
ROPE_DIM = 64
NOPE_DIM = 128
NORM_EPS = 1e-6
ROPE_BASE = 10000.0


def rope_tables(positions):
    half_dim = ROPE_DIM // 2
    inv_freq = ROPE_BASE ** (-jnp.arange(half_dim, dtype=jnp.float32) / half_dim)
    angles = positions.astype(jnp.float32)[..., None] * inv_freq
    return jnp.cos(angles), jnp.sin(angles)


def apply_rope(values, cos_tab, sin_tab):
    half_dim = ROPE_DIM // 2
    first = values[..., :half_dim]
    second = values[..., half_dim:]
    return jnp.concatenate([first * cos_tab - second * sin_tab, second * cos_tab + first * sin_tab], axis=-1)


def chunk_project(hidden, pre_len, w_q, w_dkv, g_kv, w_uk):
    req_count, chunk_len, d_model = hidden.shape
    head_count = w_uk.shape[1]
    x_rows = hidden.reshape(req_count * chunk_len, d_model)
    q_all = jnp.dot(x_rows, w_q, preferred_element_type=jnp.float32).astype(jnp.bfloat16)
    q_all = q_all.reshape(req_count, chunk_len, head_count, NOPE_DIM + ROPE_DIM)
    kv_lat = jnp.dot(x_rows, w_dkv, preferred_element_type=jnp.float32).reshape(req_count, chunk_len, LATENT + ROPE_DIM)
    lat_part = kv_lat[..., :LATENT]
    inv_rms = lax.rsqrt(jnp.mean(lat_part * lat_part, axis=-1, keepdims=True) + NORM_EPS)
    c_new = (lat_part * inv_rms * g_kv.astype(jnp.float32)).astype(jnp.bfloat16)
    cos_tab, sin_tab = rope_tables(pre_len[:, None] + jnp.arange(chunk_len)[None, :])
    kr_new = apply_rope(kv_lat[..., LATENT:], cos_tab, sin_tab).astype(jnp.bfloat16)
    q_rope = apply_rope(q_all[..., NOPE_DIM:].astype(jnp.float32), cos_tab[:, :, None, :], sin_tab[:, :, None, :]).astype(jnp.bfloat16)
    q_lat = jnp.einsum("rchn,lhn->rchl", q_all[..., :NOPE_DIM], w_uk, preferred_element_type=jnp.float32).astype(jnp.bfloat16)
    return jnp.concatenate([q_lat, q_rope], axis=-1), jnp.concatenate([c_new, kr_new], axis=-1)


def finish(o_lat, hidden, w_uv, w_o):
    req_count, chunk_len, d_model = hidden.shape
    o_heads = jnp.einsum("rhcl,lhv->rchv", o_lat, w_uv, preferred_element_type=jnp.float32).astype(jnp.bfloat16)
    attn_out = jnp.dot(o_heads.reshape(req_count * chunk_len, -1), w_o, preferred_element_type=jnp.float32)
    y_rows = hidden.reshape(req_count * chunk_len, d_model).astype(jnp.float32) + attn_out
    return y_rows.astype(jnp.bfloat16).reshape(req_count, chunk_len, d_model)


def attend(q_cat, new_keys, prefix_keys, pre_len, hidden, w_uv, w_o):
    chunk_len = q_cat.shape[1]
    prefix_max = prefix_keys.shape[1]
    score_scale = (NOPE_DIM + ROPE_DIM) ** -0.5
    s_pre = jnp.einsum("rchk,rjk->rhcj", q_cat, prefix_keys, preferred_element_type=jnp.float32) * score_scale
    s_new = jnp.einsum("rchk,rjk->rhcj", q_cat, new_keys, preferred_element_type=jnp.float32) * score_scale
    pre_mask = (jnp.arange(prefix_max)[None, :] < pre_len[:, None])[:, None, None, :]
    causal = jnp.arange(chunk_len)[None, :] <= jnp.arange(chunk_len)[:, None]
    s_pre = jnp.where(pre_mask, s_pre, -jnp.inf)
    s_new = jnp.where(causal, s_new, -jnp.inf)
    row_max = jnp.maximum(jnp.max(s_pre, axis=-1, keepdims=True), jnp.max(s_new, axis=-1, keepdims=True))
    e_pre = jnp.exp(s_pre - row_max)
    e_new = jnp.exp(s_new - row_max)
    denom_sum = jnp.sum(e_pre, axis=-1, keepdims=True) + jnp.sum(e_new, axis=-1, keepdims=True)
    o_lat = jnp.einsum("rhcj,rjl->rhcl", (e_pre / denom_sum).astype(jnp.bfloat16), prefix_keys[..., :LATENT], preferred_element_type=jnp.float32)
    o_lat = o_lat + jnp.einsum("rhcj,rjl->rhcl", (e_new / denom_sum).astype(jnp.bfloat16), new_keys[..., :LATENT], preferred_element_type=jnp.float32)
    return finish(o_lat.astype(jnp.bfloat16), hidden, w_uv, w_o)


def slot_positions(owners, pool_size, slot_count):
    dev_ids = jnp.arange(pool_size, dtype=jnp.int32)
    owner_hits = (owners[:, None] == dev_ids[None, :]).astype(jnp.int32)
    earlier = jnp.cumsum(owner_hits, axis=0) - owner_hits
    slot_rank = jnp.sum(earlier * owner_hits, axis=1)
    return jnp.where(owners >= 0, owners * slot_count + slot_rank, pool_size * slot_count)


def write_new_pages(new_keys, wr_table, cache_c, cache_kr, pool_size):
    cache_pages = cache_c.shape[1]
    write_count = wr_table.shape[0] * wr_table.shape[1]
    write_slots = -(-write_count // pool_size)
    write_pos = slot_positions(wr_table[:, :, 0].reshape(write_count), pool_size, write_slots)
    new_pages = new_keys.reshape(write_count, PAGE_LEN, LATENT + ROPE_DIM)
    out_pages = jnp.zeros((pool_size * write_slots, PAGE_LEN, LATENT + ROPE_DIM), jnp.bfloat16).at[write_pos].set(new_pages)
    out_ids = jnp.full((pool_size * write_slots,), cache_pages, jnp.int32).at[write_pos].set(wr_table[:, :, 1].reshape(write_count))
    in_pages = lax.all_to_all(out_pages, "pool", 0, 0, tiled=True)
    in_ids = lax.all_to_all(out_ids, "pool", 0, 0, tiled=True)
    cache_c_out = cache_c[0].at[in_ids].set(in_pages[..., :LATENT], mode="drop")[None]
    cache_kr_out = cache_kr[0].at[in_ids].set(in_pages[..., LATENT:], mode="drop")[None]
    return cache_c_out, cache_kr_out


def solution(mesh):
    pool_size = mesh.shape["pool"]

    def device_step(hidden, pre_len, pre_table, wr_table, cache_c, cache_kr, w_q, w_dkv, g_kv, w_uk, w_uv, w_o):
        req_count = hidden.shape[0]
        table_pages = pre_table.shape[1]
        entries = req_count * table_pages
        read_slots = max(1, (2 * entries) // pool_size)
        q_cat, new_keys = chunk_project(hidden, pre_len, w_q, w_dkv, g_kv, w_uk)
        read_pos = slot_positions(pre_table[:, :, 0].reshape(entries), pool_size, read_slots)
        asked_ids = jnp.zeros((pool_size * read_slots,), jnp.int32).at[read_pos].set(pre_table[:, :, 1].reshape(entries), mode="drop")
        served_ids = lax.all_to_all(asked_ids, "pool", 0, 0, tiled=True)
        served = jnp.concatenate([cache_c[0][served_ids], cache_kr[0][served_ids]], axis=-1)
        fetched = lax.all_to_all(served, "pool", 0, 0, tiled=True)
        prefix_keys = fetched[jnp.minimum(read_pos, pool_size * read_slots - 1)]
        prefix_keys = prefix_keys.reshape(req_count, table_pages * PAGE_LEN, LATENT + ROPE_DIM)
        cache_c_out, cache_kr_out = write_new_pages(new_keys, wr_table, cache_c, cache_kr, pool_size)
        hidden_out = attend(q_cat, new_keys, prefix_keys, pre_len, hidden, w_uv, w_o)
        return hidden_out, cache_c_out, cache_kr_out

    row_spec = P("pool")
    rep_spec = P()
    return jax.shard_map(device_step, mesh=mesh, in_specs=(row_spec,) * 6 + (rep_spec,) * 6, out_specs=(row_spec, row_spec, row_spec), check_vma=False)
```

profile of v0, /device:TPU:3, one launch (start us, length us, event | category | flops | bytes accessed | tf_op | source)
XLA Modules:
  0.0 509.4 jit_solution(1494493988980286148)
XLA Ops:
  0.7 4.8 copy.106
  5.5 0.6 fusion.64
  8.0 0.6 all_to_all.28
  8.7 0.5 constant_dynamic-update-slice_fusion
  9.2 6.4 %all-to-all-start.2 = ((s32[32,1,1]{2,1,0:T(1,128)}), s32[32,1,1]{2,1,0:T(1,128)S(1)}, u32[]{:S(2)}, u32[]{:S(2)}) async-start(s32[32,1,1]{2,1,0:T(1,128)} %constant_dynamic-update-slice_fusion), calls=%async_computation.2 | async-start | bytes 32768 | tf_op jit(solution)/shard_map/all_to_all | solution.py:89
  16.7 5.9 %convolution_bitcast_fusion = f32[1,64,576]{2,1,0:T(8,128)S(1)} fusion(bf16[7168,576]{0,1:T(8,128)(2,1)} %param.23, bf16[1,64,7168]{2,1,0:T(8,128)(2,1)S(1)} %copy-done), kind=kOutput, calls=%fused_computation.41 | convolution fusion | flops 528482304 | bytes 9322496 | tf_op jit(solution)/shard_map/dot_general | solution.py:34
  23.1 0.7 and_reduce_fusion
  23.8 0.8 scatter_custom_fusion
  24.6 0.7 all_to_all.24
  25.3 5.8 %all-to-all-start = ((s32[32,4,1]{1,2,0:T(1,128)}), s32[32,4,1]{1,2,0:T(1,128)S(1)}, u32[]{:S(2)}, u32[]{:S(2)}) async-start(s32[32,4,1]{1,2,0:T(1,128)} %bitcast.9), calls=%async_computation | async-start | bytes 32768 | tf_op jit(solution)/shard_map/all_to_all | solution.py:106
  31.2 1.9 broadcast_in_dim.31
  33.1 1.2 fusion.41
  34.3 2.5 all-to-all-done
  36.8 4.8 all-to-all-start.3
  41.6 1.9 copy.49
  43.6 0.5 broadcast.378
  44.1 0.7 reduce.19
  44.9 2.1 gather_fusion.1
  47.0 8.5 %gather_fusion = bf16[128,64,512]{2,1,0:T(8,128)(2,1)} fusion(bf16[65,64,512]{2,1,0:T(8,128)(2,1)} %bitcast.143, s32[1024]{0:T(1024)S(1)} %pad_clamp_fusion.1), kind=kCustom, calls=%fused_computation | custom fusion | bytes 16777728 | tf_op jit(solution)/shard_map/gather | solution.py:107
  55.6 9.7 %pad_maximum_fusion = bf16[128,64,576]{2,1,0:T(8,128)(2,1)} fusion(bf16[128,64,64]{2,1,0:T(8,128)(2,1)} %gather_fusion.1, bf16[128,64,512]{2,1,0:T(8,128)(2,1)} %gather_fusion), kind=kLoop, calls=%fused_computation.15 | loop fusion | flops 18874368 | bytes 18874368 | tf_op jit(solution)/shard_map/concatenate | solution.py:107
  65.3 36.4 %all-to-all-done.3 = bf16[32,64,576]{2,1,0:T(8,128)(2,1)} async-done(((bf16[32,64,576]{2,1,0:T(8,128)(2,1)}), bf16[32,64,576]{2,1,0:T(8,128)(2,1)}, u32[]{:S(2)}, u32[]{:S(2)}) %all-to-all-start.3) | async-done | bytes 2359328 | tf_op jit(solution)/shard_map/all_to_all | solution.py:88
  101.7 15.8 %all-to-all-start.1 = ((bf16[128,64,576]{2,1,0:T(8,128)(2,1)}), bf16[128,64,576]{2,1,0:T(8,128)(2,1)}, u32[]{:S(2)}, u32[]{:S(2)}) async-start(bf16[128,64,576]{2,1,0:T(8,128)(2,1)} %pad_maximum_fusion), calls=%async_computation.1 | async-start | bytes 20971520 | tf_op jit(solution)/shard_map/all_to_all | solution.py:108
  117.5 57.3 %convolution_convert_fusion = bf16[64,12288]{1,0:T(8,128)(2,1)} fusion(bf16[7168,12288]{1,0:T(8,128)(2,1)} %param.22, bf16[1,64,7168]{2,1,0:T(8,128)(2,1)S(1)} %copy-done), kind=kOutput, calls=%fused_computation.14 | convolution fusion | flops 11275075584 | bytes 178651136 | tf_op jit(solution)/shard_map/dot_general | solution.py:32
  174.8 3.6 reshape.562
  178.4 0.2 slice.93
  179.0 0.6 copy_convert_fusion
  179.7 0.8 subtract_convert_fusion
  180.5 22.0 %convert_bitcast_fusion = bf16[1,64,64,512]{3,1,2,0:T(8,128)(2,1)S(1)} fusion(bf16[512,64,128]{2,1,0:T(8,128)(2,1)} %param.25, bf16[1,64,64,128]{3,2,1,0:T(8,128)(2,1)S(1)} %slice.93), kind=kOutput, calls=%fused_computation.31 | convolution fusion | flops 538968064 | bytes 13631488 | tf_op jit(solution)/shard_map/rchn,lhn->rchl/dot_general | solution.py:41
  202.5 1.0 maximum_bitcast_fusion
  203.5 2.3 copy-done.2
  205.9 6.8 %fusion.18 = (f32[64,64]{0,1:T(8,128)S(1)}, f32[64,64,64]{2,0,1:T(8,128)S(1)}) fusion(pred[64,64]{1,0:T(8,128)(4,1)S(1)} %iota_compare_fusion, bf16[64,64,576]{2,0,1:T(8,128)(2,1)S(1)} %maximum_bitcast_fusion, bf16[1,64,32]{2,1,0:T(8,128)(2,1)S(1)} %get-tuple-element.41, bf16[1,64,32]{2,1,0:T(8,128)(2,1)S(1)} %get-tuple-element.40, ...), kind=kOutput, calls=%fused_computation.38 | convolution fusion | flops 302993408 | bytes 5861376 | tf_op jit(solution)/shard_map/rchk,rjk->rhcj/dot_general | solution.py:58
  212.7 0.7 reduce.15
  213.4 1.9 slice.102
  215.2 3.4 scatter_fusion.1
  218.7 2.1 copy.61
  220.8 3.2 slice.101
  224.0 6.0 %scatter_fusion = bf16[65,64,512]{2,1,0:T(8,128)(2,1)} fusion(bf16[65,64,512]{2,1,0:T(8,128)(2,1)} %bitcast.144, s32[32]{0:T(128)S(1)} %fusion.56, bf16[32,64,512]{2,1,0:T(8,128)(2,1)} %slice.101), kind=kCustom, calls=%fused_computation.4 | custom fusion | bytes 6291584 | tf_op jit(solution)/shard_map/scatter | solution.py:90
  230.0 116.7 %all-to-all-done.1 = bf16[128,64,576]{2,1,0:T(8,128)(2,1)} async-done(((bf16[128,64,576]{2,1,0:T(8,128)(2,1)}), bf16[128,64,576]{2,1,0:T(8,128)(2,1)}, u32[]{:S(2)}, u32[]{:S(2)}) %all-to-all-start.1) | async-done | bytes 9437216 | tf_op jit(solution)/shard_map/all_to_all | solution.py:108
  346.7 7.6 %gather_fusion.2 = bf16[64,64,576]{2,1,0:T(8,128)(2,1)} fusion(bf16[128,64,576]{2,1,0:T(8,128)(2,1)} %all-to-all-done.1, s32[1024]{0:T(1024)S(1)} %pad_clamp_fusion), kind=kCustom, calls=%fused_computation.2 | custom fusion | bytes 9437440 | tf_op jit(solution)/shard_map/gather | solution.py:109
  354.3 36.3 %bitcast_reduce_fusion = (f32[64,64]{0,1:T(8,128)S(1)}, f32[4096,64,64]{0,2,1:T(8,128)}) fusion(pred[4096]{0:T(1024)(128)(4,1)S(1)} %iota_compare_fusion.2, bf16[4096,576,1]{1,0,2:T(8,128)(2,1)} %bitcast.149, bf16[64,64,576]{2,0,1:T(8,128)(2,1)} %copy-done.2), kind=kOutput, calls=%fused_computation.7 | convolution fusion | flops 19377680384 | bytes 76566528 | tf_op jit(solution)/shard_map/rchk,rjk->rhcj/dot_general | solution.py:57
  390.5 0.8 fusion.17
  391.3 21.4 %fusion.1 = f32[64,64]{0,1:T(8,128)S(1)} fusion(f32[4096,64,64]{0,2,1:T(8,128)} %get-tuple-element.49, f32[64,64]{0,1:T(8,128)S(1)} %max.8, pred[4096]{0:T(1024)(128)(4,1)S(1)} %iota_compare_fusion.2), kind=kLoop, calls=%fused_computation.11 | loop fusion | flops 67104768 | bytes 67145728 | tf_op jit(solution)/shard_map/reduce_sum | solution.py:66
  412.8 29.8 %fusion.2 = f32[64,64,512]{2,0,1:T(8,128)} fusion(f32[4096,64,64]{0,2,1:T(8,128)} %get-tuple-element.49, f32[64,64]{0,1:T(8,128)S(1)} %add.123, f32[64,64]{0,1:T(8,128)S(1)} %max.8, pred[4096]{0:T(1024)(128)(4,1)S(1)} %iota_compare_fusion.2, bf16[1,4096,576]{2,1,0:T(8,128)(2,1)} %bitcast.150), kind=kOutput, calls=%fused_computation.12 | convolution fusion | flops 17263755264 | bytes 79728640 | tf_op jit(solution)/shard_map/rhcj,rjl->rhcl/dot_general | solution.py:67
  442.5 5.5 %add_convert_fusion = bf16[64,64,512]{2,0,1:T(8,128)(2,1)S(1)} fusion(f32[64,64,512]{2,0,1:T(8,128)} %fusion.2, f32[64,64,64]{2,0,1:T(8,128)S(1)} %get-tuple-element.51, f32[64,64]{0,1:T(8,128)S(1)} %add.123, f32[64,64]{0,1:T(8,128)S(1)} %max.8, pred[64,64]{1,0:T(8,128)(4,1)S(1)} %iota_compare_fusion, bf16[1,64,512]{2,1,0:T(8,128)(2,1)S(1)} %copy-done.5), kind=kOutput, calls=%fused_computation.20 | convolution fusion | flops 273940480 | bytes 13733888 | tf_op jit(solution)/shard_map/rhcj,rjl->rhcl/dot_general | solution.py:68
  448.0 0.4 copy-done.10
  448.4 19.6 %fusion.24 = bf16[1,64,64,128]{3,1,2,0:T(8,128)(2,1)S(1)} fusion(bf16[512,64,128]{2,1,0:T(8,128)(2,1)S(1)} %copy-done.10, bf16[64,64,512]{2,0,1:T(8,128)(2,1)S(1)} %add_convert_fusion), kind=kOutput, calls=%fused_computation.40 | convolution fusion | flops 537395200 | bytes 13631488 | tf_op jit(solution)/shard_map/rhcl,lhv->rchv/dot_general | solution.py:47
  468.0 0.7 copy.60
  468.7 40.5 %fusion.9 = bf16[1,64,7168]{2,1,0:T(8,128)(2,1)} fusion(bf16[8192,7168]{1,0:T(8,128)(2,1)} %param.27, bf16[8,8,64,128]{3,2,1,0:T(8,128)(2,1)S(1)} %bitcast.151, bf16[1,64,7168]{2,1,0:T(8,128)(2,1)S(1)} %copy-done.1), kind=kOutput, calls=%fused_computation.23 | convolution fusion | flops 7517569024 | bytes 120324096 | tf_op jit(solution)/shard_map/dot_general | solution.py:48
  (46 shorter events, 1.5 us)
Async XLA Ops:
  0.6 16.1 %copy-start = (bf16[1,64,7168]{2,1,0:T(8,128)(2,1)S(1)}, bf16[1,64,7168]{2,1,0:T(8,128)(2,1)}, u32[]{:S(2)}) copy-start(bf16[1,64,7168]{2,1,0:T(8,128)(2,1)} %param.16) | copy-start | bytes 2752516
  0.6 15.6 %copy-start.6 = (s32[1,64,2]{1,2,0:T(2,128)S(1)}, s32[1,64,2]{1,2,0:T(2,128)}, u32[]{:S(2)}) copy-start(s32[1,64,2]{1,2,0:T(2,128)} %param.18) | copy-start | bytes 1540
  0.7 4.8 copy-start.7
  0.7 15.6 %copy-start.8 = (bf16[512]{0:T(512)(128)(2,1)S(1)}, bf16[512]{0:T(512)(128)(2,1)}, u32[]{:S(2)}) copy-start(bf16[512]{0:T(512)(128)(2,1)} %param.24) | copy-start | bytes 3076
  5.5 17.6 %copy-start.9 = (s32[3]{0:T(128)S(1)}, s32[3]{0:T(128)}, u32[]{:S(2)}) copy-start(s32[3]{0:T(128)} %constant.90.clone.1) | copy-start | bytes 40
  9.2 16.2 %all-to-all-start.2 = ((s32[32,1,1]{2,1,0:T(1,128)}), s32[32,1,1]{2,1,0:T(1,128)S(1)}, u32[]{:S(2)}, u32[]{:S(2)}) async-start(s32[32,1,1]{2,1,0:T(1,128)} %constant_dynamic-update-slice_fusion), calls=%async_computation.2 | async-start | bytes 32768 | tf_op jit(solution)/shard_map/all_to_all | solution.py:89
  22.6 19.0 %copy-start.3 = (bf16[1,65,64,64]{1,3,2,0:T(8,128)(2,1)S(1)}, bf16[1,65,64,64]{1,3,2,0:T(8,128)(2,1)}, u32[]{:S(2)}) copy-start(bf16[1,65,64,64]{1,3,2,0:T(8,128)(2,1)} %param.21) | copy-start | bytes 1597444
  23.0 180.5 %copy-start.4 = (bf16[1,64,512]{2,1,0:T(8,128)(2,1)}, bf16[1,64,512]{2,1,0:T(8,128)(2,1)S(1)}, u32[]{:S(2)}) copy-start(bf16[1,64,512]{2,1,0:T(8,128)(2,1)S(1)} %multiply_convert_fusion) | copy-start | bytes 196612
  25.3 11.5 %all-to-all-start = ((s32[32,4,1]{1,2,0:T(1,128)}), s32[32,4,1]{1,2,0:T(1,128)S(1)}, u32[]{:S(2)}, u32[]{:S(2)}) async-start(s32[32,4,1]{1,2,0:T(1,128)} %bitcast.9), calls=%async_computation | async-start | bytes 32768 | tf_op jit(solution)/shard_map/all_to_all | solution.py:106
  36.8 64.9 %all-to-all-start.3 = ((bf16[32,64,576]{2,1,0:T(8,128)(2,1)}), bf16[32,64,576]{2,1,0:T(8,128)(2,1)}, u32[]{:S(2)}, u32[]{:S(2)}) async-start(bf16[32,64,576]{2,1,0:T(8,128)(2,1)} %fusion.41), calls=%async_computation.3 | async-start | bytes 5242880 | tf_op jit(solution)/shard_map/all_to_all | solution.py:88
  101.7 245.0 %all-to-all-start.1 = ((bf16[128,64,576]{2,1,0:T(8,128)(2,1)}), bf16[128,64,576]{2,1,0:T(8,128)(2,1)}, u32[]{:S(2)}, u32[]{:S(2)}) async-start(bf16[128,64,576]{2,1,0:T(8,128)(2,1)} %pad_maximum_fusion), calls=%async_computation.1 | async-start | bytes 20971520 | tf_op jit(solution)/shard_map/all_to_all | solution.py:108
  203.5 2.3 copy-start.2
  412.8 29.8 %copy-start.5 = (bf16[1,64,512]{2,1,0:T(8,128)(2,1)S(1)}, bf16[1,64,512]{2,1,0:T(8,128)(2,1)}, u32[]{:S(2)}) copy-start(bf16[1,64,512]{2,1,0:T(8,128)(2,1)} %copy-done.4) | copy-start | bytes 196612
  442.5 5.8 %copy-start.10 = (bf16[512,64,128]{2,1,0:T(8,128)(2,1)S(1)}, bf16[512,64,128]{2,1,0:T(8,128)(2,1)}, u32[]{:S(2)}) copy-start(bf16[512,64,128]{2,1,0:T(8,128)(2,1)} %param.26) | copy-start | bytes 25165828
  448.4 20.3 %copy-start.1 = (bf16[1,64,7168]{2,1,0:T(8,128)(2,1)S(1)}, bf16[1,64,7168]{2,1,0:T(8,128)(2,1)}, u32[]{:S(2)}) copy-start(bf16[1,64,7168]{2,1,0:T(8,128)(2,1)} %param.16) | copy-start | bytes 2752516
where the time goes:
time: 516 us; the launch traced here: 509 us
  matrix products  224 us (43%)
  waiting for transfers between devices  156 us (30%)
  local copies, waits for them, and re-layouts  54.8 us (11%)
  other arithmetic  38.7 us (8%)
  starting transfers between devices  32.8 us (6%)
    all_to_all x1, waiting for transfers between devices, device_step(): fetched = lax.all_to_all(served, 'pool', 0, 0, tiled=True)  117 us
    dot_general x1, matrix products, chunk_project(): jnp.dot(x_rows, w_q, preferred_element_type=jnp.float32)  57.3 us
    dot_general x1, matrix products, finish(): jnp.dot(o_heads.reshape(req_count * chunk_len, -1), w_o, preferred_elemen...  40.5 us
    all_to_all x1, waiting for transfers between devices, write_new_pages(): in_pages = lax.all_to_all(out_pages, 'pool', 0, 0, tiled=True)  36.4 us
    dot_general x1, matrix products, attend(): jnp.einsum('rchk,rjk->rhcj', q_cat, prefix_keys, preferred_element_type=j...  36.3 us
    dot_general x1, matrix products, attend(): jnp.einsum('rhcj,rjl->rhcl', (e_pre / denom_sum).astype(jnp.bfloat16), pr...  29.8 us
    dot_general x1, matrix products, chunk_project(): jnp.einsum('rchn,lhn->rchl', q_all[..., :NOPE_DIM], w_uk, preferred_eleme...  22 us
    reduce_sum x1, other arithmetic, attend(): jnp.sum(e_pre, axis=-1, keepdims=True)  21.4 us
  transfers between devices with their start and end apart: 4, of which 3 were waited for; matrix products, arithmetic and copies ran while one was open for 28% of the time, Pallas kernels for 0%

commit v1 on v0

v1 whole, which is shorter than its diff:
```python
import functools

import jax
import jax.numpy as jnp
from jax import lax
from jax.experimental import pallas as pl
from jax.experimental.pallas import tpu as pltpu
from jax.sharding import PartitionSpec as P

PAGE_LEN = 64
LATENT = 512
ROPE_DIM = 64
NOPE_DIM = 128
HEADS = 64
CHUNK = 64
D_MODEL = 7168
SLOTS = 4
NORM_EPS = 1e-6
ROPE_BASE = 10000.0
MESH = pl.DeviceIdType.MESH
VMEM_LIMIT = 62 * 1024 * 1024


def rope_tables(positions):
    half_dim = ROPE_DIM // 2
    inv_freq = ROPE_BASE ** (-jnp.arange(half_dim, dtype=jnp.float32) / half_dim)
    angles = positions.astype(jnp.float32)[..., None] * inv_freq
    return jnp.cos(angles), jnp.sin(angles)


def apply_rope(values, cos_tab, sin_tab):
    half_dim = ROPE_DIM // 2
    first = values[..., :half_dim]
    second = values[..., half_dim:]
    return jnp.concatenate([first * cos_tab - second * sin_tab, second * cos_tab + first * sin_tab], axis=-1)


def exchange_kernel(n, ids_ref, x_ref, cache_c, cache_kr, w_q, got_c, got_k, q_ref,
                    ids_in, ids_smem, cc, ck, kp, stage_c, stage_k, wbuf,
                    loc_sem, id_send, id_recv, c_send, c_recv, k_send, k_recv, w_sem, out_sem):
    me = lax.axis_index("pool")
    pages = kp.shape[0]
    blk = wbuf.shape[2]
    n_blk = w_q.shape[1] // blk

    load_c = pltpu.make_async_copy(cache_c.at[pl.ds(0, pages)], cc, loc_sem.at[0])
    load_k = pltpu.make_async_copy(cache_kr.at[pl.ds(0, pages)], ck, loc_sem.at[1])
    load_c.start()
    load_k.start()

    def peer_of(j):
        off = (j + 1) // 2
        sign = 1 - 2 * (j % 2)
        return (me + n // 2 + sign * off + n) % n

    barrier = pltpu.get_barrier_semaphore()

    @pl.loop(0, n - 1)
    def _(j):
        pl.semaphore_signal(barrier, inc=1, device_id=(peer_of(j),), device_id_type=MESH)

    def w_copy(i, slot):
        return pltpu.make_async_copy(w_q.at[:, pl.ds(pl.multiple_of(i * blk, blk), blk)], wbuf.at[slot], w_sem.at[slot])

    w_copy(0, 0).start()
    w_copy(1, 1).start()
    pl.semaphore_wait(barrier, n - 1)

    def id_copy(peer, src):
        return pltpu.make_async_remote_copy(src_ref=ids_ref.at[peer], dst_ref=ids_in.at[src], send_sem=id_send.at[peer],
                                            recv_sem=id_recv.at[src], device_id=(peer,), device_id_type=MESH)

    @pl.loop(0, n - 1)
    def _(j):
        id_copy(peer_of(j), me).start()

    own_ids = pltpu.make_async_copy(ids_ref.at[me], ids_in.at[me], loc_sem.at[2])
    own_ids.start()

    load_k.wait()

    @pl.loop(0, pages)
    def _(i):
        page = ck[i]
        kp[i] = jnp.concatenate([page[: PAGE_LEN // 2], page[PAGE_LEN // 2:]], axis=-1)

    load_c.wait()
    own_ids.wait()

    @pl.loop(0, n - 1)
    def _(j):
        id_copy(peer_of(j), peer_of(j)).wait_recv()

    to_smem = pltpu.make_async_copy(ids_in, ids_smem, loc_sem.at[3])
    to_smem.start()
    to_smem.wait()

    def c_copy(peer, src):
        return pltpu.make_async_remote_copy(src_ref=stage_c.at[peer], dst_ref=got_c.at[src], send_sem=c_send.at[peer],
                                            recv_sem=c_recv.at[src], device_id=(peer,), device_id_type=MESH)

    def k_copy(peer, src):
        return pltpu.make_async_remote_copy(src_ref=stage_k.at[peer], dst_ref=got_k.at[src], send_sem=k_send.at[peer],
                                            recv_sem=k_recv.at[src], device_id=(peer,), device_id_type=MESH)

    def fill(peer):
        for s in range(SLOTS):
            page = ids_smem[peer, 0, s]
            stage_c[peer, s] = cc[page]
            stage_k[peer, s] = kp[page]

    @pl.loop(0, n - 1)
    def _(j):
        peer = peer_of(j)
        fill(peer)
        c_copy(peer, me).start()
        k_copy(peer, me).start()

    fill(me)
    own_c = pltpu.make_async_copy(stage_c.at[me], got_c.at[me], out_sem.at[0])
    own_k = pltpu.make_async_copy(stage_k.at[me], got_k.at[me], out_sem.at[1])
    own_c.start()
    own_k.start()

    @pl.loop(0, n_blk // 2)
    def _(g):
        for slot in range(2):
            i = g * 2 + slot
            w_copy(i, slot).wait()
            part = jnp.dot(x_ref[...], wbuf[slot], preferred_element_type=jnp.float32)
            q_ref[:, pl.ds(pl.multiple_of(i * blk, blk), blk)] = part.astype(jnp.bfloat16)

            @pl.when(i + 2 < n_blk)
            def _():
                w_copy(i + 2, slot).start()

    own_c.wait()
    own_k.wait()

    @pl.loop(0, n - 1)
    def _(j):
        peer = peer_of(j)
        id_copy(peer, me).wait_send()
        c_copy(peer, peer).wait()
        k_copy(peer, peer).wait()


def exchange(n, ids, x, cache_c, cache_kr, w_q):
    pages = cache_c.shape[0] - 1
    blk = 256
    any_spec = pl.BlockSpec(memory_space=pl.ANY)
    vmem_spec = pl.BlockSpec(memory_space=pltpu.VMEM)
    return pl.pallas_call(
        functools.partial(exchange_kernel, n),
        name="exchange",
        out_shape=(
            jax.ShapeDtypeStruct((n, SLOTS, PAGE_LEN, LATENT), jnp.bfloat16),
            jax.ShapeDtypeStruct((n, SLOTS, PAGE_LEN // 2, 2 * ROPE_DIM), jnp.bfloat16),
            jax.ShapeDtypeStruct((CHUNK, w_q.shape[1]), jnp.bfloat16),
        ),
        in_specs=[vmem_spec, vmem_spec, any_spec, any_spec, any_spec],
        out_specs=(any_spec, any_spec, vmem_spec),
        scratch_shapes=[
            pltpu.VMEM((n, 1, 128), jnp.int32),
            pltpu.SMEM((n, 1, 128), jnp.int32),
            pltpu.VMEM((pages, PAGE_LEN, LATENT), jnp.bfloat16),
            pltpu.VMEM((pages, PAGE_LEN, ROPE_DIM), jnp.bfloat16),
            pltpu.VMEM((pages, PAGE_LEN // 2, 2 * ROPE_DIM), jnp.bfloat16),
            pltpu.VMEM((n, SLOTS, PAGE_LEN, LATENT), jnp.bfloat16),
            pltpu.VMEM((n, SLOTS, PAGE_LEN // 2, 2 * ROPE_DIM), jnp.bfloat16),
            pltpu.VMEM((2, D_MODEL, blk), jnp.bfloat16),
            pltpu.SemaphoreType.DMA((4,)),
            pltpu.SemaphoreType.DMA((n,)),
            pltpu.SemaphoreType.DMA((n,)),
            pltpu.SemaphoreType.DMA((n,)),
            pltpu.SemaphoreType.DMA((n,)),
            pltpu.SemaphoreType.DMA((n,)),
            pltpu.SemaphoreType.DMA((n,)),
            pltpu.SemaphoreType.DMA((2,)),
            pltpu.SemaphoreType.DMA((2,)),
        ],
        compiler_params=pltpu.CompilerParams(collective_id=0, has_side_effects=True, vmem_limit_bytes=VMEM_LIMIT),
    )(ids, x, cache_c, cache_kr, w_q)


def slot_positions(owners, pool_size, slot_count):
    dev_ids = jnp.arange(pool_size, dtype=jnp.int32)
    owner_hits = (owners[:, None] == dev_ids[None, :]).astype(jnp.int32)
    tri = (jnp.arange(owners.shape[0])[:, None] > jnp.arange(owners.shape[0])[None, :]).astype(jnp.float32)
    earlier = jnp.dot(tri, owner_hits.astype(jnp.float32)).astype(jnp.int32)
    slot_rank = jnp.sum(earlier * owner_hits, axis=1)
    return jnp.where(owners >= 0, owners * slot_count + slot_rank, pool_size * slot_count)


def attend_kernel(keys_tile, valid_ref, qc_ref, qk_ref, got_c, got_k, newc_ref, newk_ref, o_ref, m_ref, l_ref, acc_ref, cbuf, kbuf, sem):
    scale = (NOPE_DIM + ROPE_DIM) ** -0.5
    count = valid_ref[0]
    per = keys_tile // PAGE_LEN
    rows = qc_ref.shape[0]
    n_tiles = (count + per - 1) // per

    def copies(t, slot, s):
        page = valid_ref[1 + jnp.minimum(t * per + s, count - 1)]
        return (pltpu.make_async_copy(got_c.at[page], cbuf.at[slot, s], sem.at[slot, s, 0]),
                pltpu.make_async_copy(got_k.at[page], kbuf.at[slot, s], sem.at[slot, s, 1]))

    def start(t, slot):
        for s in range(per):
            for c in copies(t, slot, s):
                c.start()

    def scores(qc, qk, ck, kk):
        dims = (((1,), (1,)), ((), ()))
        s = lax.dot_general(qc, ck, dims, preferred_element_type=jnp.float32)
        return (s + lax.dot_general(qk, kk, dims, preferred_element_type=jnp.float32)) * scale

    @pl.when(n_tiles > 0)
    def _():
        start(0, 0)

    causal = (lax.broadcasted_iota(jnp.int32, (rows, CHUNK), 1) <= lax.broadcasted_iota(jnp.int32, (rows, CHUNK), 0) % CHUNK)
    s = scores(qc_ref[...], qk_ref[:, :ROPE_DIM], newc_ref[...], newk_ref[...])
    s = jnp.where(causal, s, -jnp.inf)
    m = jnp.max(s, axis=-1, keepdims=True)
    p = jnp.exp(s - m)
    m_ref[...] = jnp.broadcast_to(m, m_ref.shape)
    l_ref[...] = jnp.broadcast_to(jnp.sum(p, axis=-1, keepdims=True), l_ref.shape)
    acc_ref[...] = jnp.dot(p.astype(jnp.bfloat16), newc_ref[...], preferred_element_type=jnp.float32)

    low = lax.broadcasted_iota(jnp.int32, (PAGE_LEN // 2, 2 * ROPE_DIM), 1) < ROPE_DIM

    def body(t, _):
        slot = lax.rem(t, 2)

        @pl.when(t + 1 < n_tiles)
        def _():
            start(t + 1, 1 - slot)

        for s in range(per):
            for c in copies(t, slot, s):
                c.wait()
        ck = cbuf[slot].reshape(keys_tile, LATENT)
        parts = []
        for s in range(per):
            page = kbuf[slot, s]
            zero = jnp.zeros_like(page)
            parts += [jnp.where(low, page, zero), jnp.where(low, zero, page)]
        kk = jnp.concatenate(parts, axis=0)
        sc = scores(qc_ref[...], qk_ref[...], ck, kk)
        key_ids = t * keys_tile + lax.broadcasted_iota(jnp.int32, sc.shape, 1)
        sc = jnp.where(key_ids < count * PAGE_LEN, sc, -jnp.inf)
        m_old = m_ref[:, :1]
        m_new = jnp.maximum(m_old, jnp.max(sc, axis=-1, keepdims=True))
        alpha = jnp.exp(m_old - m_new)
        p = jnp.exp(sc - m_new)
        m_ref[...] = jnp.broadcast_to(m_new, m_ref.shape)
        l_ref[...] = l_ref[...] * alpha + jnp.sum(p, axis=-1, keepdims=True)
        acc_ref[...] = acc_ref[...] * alpha + jnp.dot(p.astype(jnp.bfloat16), ck, preferred_element_type=jnp.float32)
        return 0

    lax.fori_loop(0, n_tiles, body, 0)
    o_ref[...] = (acc_ref[...] / l_ref[:, :1]).astype(jnp.bfloat16)


def attend(valid, qc, qk, got_c, got_k, new_c, new_k):
    total = qc.shape[0]
    rows = 512
    keys_tile = 512
    per = keys_tile // PAGE_LEN
    any_spec = pl.BlockSpec(memory_space=pl.ANY)
    return pl.pallas_call(
        functools.partial(attend_kernel, keys_tile),
        name="attend",
        grid=(total // rows,),
        out_shape=jax.ShapeDtypeStruct((total, LATENT), jnp.bfloat16),
        in_specs=[
            pl.BlockSpec(memory_space=pltpu.SMEM),
            pl.BlockSpec((rows, LATENT), lambda i: (i, 0)),
            pl.BlockSpec((rows, 2 * ROPE_DIM), lambda i: (i, 0)),
            any_spec,
            any_spec,
            pl.BlockSpec((CHUNK, LATENT), lambda i: (0, 0)),
            pl.BlockSpec((CHUNK, ROPE_DIM), lambda i: (0, 0)),
        ],
        out_specs=pl.BlockSpec((rows, LATENT), lambda i: (i, 0)),
        scratch_shapes=[
            pltpu.VMEM((rows, 128), jnp.float32),
            pltpu.VMEM((rows, 128), jnp.float32),
            pltpu.VMEM((rows, LATENT), jnp.float32),
            pltpu.VMEM((2, per, PAGE_LEN, LATENT), jnp.bfloat16),
            pltpu.VMEM((2, per, PAGE_LEN // 2, 2 * ROPE_DIM), jnp.bfloat16),
            pltpu.SemaphoreType.DMA((2, per, 2)),
        ],
        compiler_params=pltpu.CompilerParams(dimension_semantics=("arbitrary",), vmem_limit_bytes=VMEM_LIMIT),
    )(valid, qc, qk, got_c, got_k, new_c, new_k)


def write_new_pages(n, new_c, new_k, write_owner, cache_c, cache_kr):
    rows = jnp.concatenate([new_c, new_k], axis=-1).reshape(n, CHUNK // n, LATENT + ROPE_DIM)
    mark = jnp.broadcast_to(write_owner, (n, 1))
    owners = lax.all_to_all(mark, "pool", 0, 0, tiled=True)[:, 0]
    parts = lax.all_to_all(rows, "pool", 0, 0, tiled=True)
    order = jnp.sum(jnp.where(owners[None, :] == jnp.arange(n)[:, None], jnp.arange(n)[None, :], 0), axis=1)
    page = lax.all_to_all(parts[order], "pool", 0, 0, tiled=True).reshape(CHUNK, LATENT + ROPE_DIM)
    out_c = lax.dynamic_update_slice(cache_c, page[None, None, :, :LATENT], (0, cache_c.shape[1] - 1, 0, 0))
    out_kr = lax.dynamic_update_slice(cache_kr, page[None, None, :, LATENT:], (0, cache_kr.shape[1] - 1, 0, 0))
    return out_c, out_kr


def solution(mesh):
    n = mesh.shape["pool"]

    def device_step(hidden, pre_len, pre_table, wr_table, cache_c, cache_kr, w_q, w_dkv, g_kv, w_uk, w_uv, w_o):
        x = hidden[0]
        owners = pre_table[0, :, 0]
        pos = slot_positions(owners, n, SLOTS)
        slot_ids = jnp.arange(n * SLOTS, dtype=jnp.int32)
        hit = pos[None, :] == slot_ids[:, None]
        asked = jnp.sum(jnp.where(hit, pre_table[0, :, 1][None, :], 0), axis=1)
        ids = jnp.pad(asked.reshape(n, 1, SLOTS), ((0, 0), (0, 0), (0, 128 - SLOTS)))
        got_c, got_k, q_all = exchange(n, ids, x, cache_c[0], cache_kr[0], w_q)
        got_c = got_c.reshape(n * SLOTS, PAGE_LEN, LATENT)
        got_k = got_k.reshape(n * SLOTS, PAGE_LEN // 2, 2 * ROPE_DIM)
        valid = jnp.concatenate([pre_len // PAGE_LEN, jnp.minimum(pos, n * SLOTS - 1)]).astype(jnp.int32)

        kv_lat = jnp.dot(x, w_dkv, preferred_element_type=jnp.float32)
        lat_part = kv_lat[:, :LATENT]
        inv_rms = lax.rsqrt(jnp.mean(lat_part * lat_part, axis=-1, keepdims=True) + NORM_EPS)
        c_new = (lat_part * inv_rms * g_kv.astype(jnp.float32)).astype(jnp.bfloat16)
        cos_tab, sin_tab = rope_tables(pre_len[0] + jnp.arange(CHUNK))
        kr_new = apply_rope(kv_lat[:, LATENT:], cos_tab, sin_tab).astype(jnp.bfloat16)
        out_c, out_kr = write_new_pages(n, c_new, kr_new, wr_table[0, 0, 0], cache_c, cache_kr)

        q_all = q_all.reshape(CHUNK, HEADS, NOPE_DIM + ROPE_DIM)
        q_rope = apply_rope(q_all[..., NOPE_DIM:].astype(jnp.float32), cos_tab[:, None, :], sin_tab[:, None, :]).astype(jnp.bfloat16)
        q_lat = jnp.einsum("chn,lhn->hcl", q_all[..., :NOPE_DIM], w_uk, preferred_element_type=jnp.float32).astype(jnp.bfloat16)
        q_rope = q_rope.transpose(1, 0, 2).reshape(HEADS * CHUNK, ROPE_DIM)
        q_dup = jnp.concatenate([q_rope, q_rope], axis=-1)
        o_lat = attend(valid, q_lat.reshape(HEADS * CHUNK, LATENT), q_dup, got_c, got_k, c_new, kr_new)
        o_lat = o_lat.reshape(HEADS, CHUNK, LATENT)
        o_heads = jnp.einsum("hcl,lhv->chv", o_lat, w_uv, preferred_element_type=jnp.float32).astype(jnp.bfloat16)
        attn_out = jnp.dot(o_heads.reshape(CHUNK, -1), w_o, preferred_element_type=jnp.float32)
        y = (x.astype(jnp.float32) + attn_out).astype(jnp.bfloat16)
        return y[None], out_c, out_kr

    row_spec = P("pool")
    rep_spec = P()
    return jax.shard_map(device_step, mesh=mesh, in_specs=(row_spec,) * 6 + (rep_spec,) * 6, out_specs=(row_spec,) * 3, check_vma=False)
```

time: 516 us -> 503 us (0.975)
  the two profiles are of different devices: /device:TPU:3 before, /device:TPU:0 now
where the time goes in v1:
time: 503 us
  Pallas kernels  319 us (63%)
  matrix products  89.3 us (18%)
  starting transfers between devices  52.8 us (10%)
  local copies, waits for them, and re-layouts  26.2 us (5%)
  other arithmetic  6.89 us (1%)
  waiting for transfers between devices  6.58 us (1%)
    pallas_call x1, Pallas kernels, exchange(): pl.pallas_call(functools.partial(exchange_kernel, n), name='exchange', ou...  209 us
    pallas_call x1, Pallas kernels, attend(): pl.pallas_call(functools.partial(attend_kernel, keys_tile), name='attend'...  110 us
    all_to_all x1, starting transfers between devices, write_new_pages(): parts = lax.all_to_all(rows, 'pool', 0, 0, tiled=True)  42.9 us
    dot_general x1, matrix products, device_step(): jnp.dot(o_heads.reshape(CHUNK, -1), w_o, preferred_element_type=jnp.float32)  40.1 us
    dot_general x1, matrix products, device_step(): jnp.einsum('hcl,lhv->chv', o_lat, w_uv, preferred_element_type=jnp.float32)  22 us
    dot_general x1, matrix products, device_step(): jnp.einsum('chn,lhn->hcl', q_all[..., :NOPE_DIM], w_uk, preferred_element...  20.6 us
  transfers between devices with their start and end apart: 3, of which 1 were waited for; matrix products, arithmetic and copies ran while one was open for 21% of the time, Pallas kernels for 63%

profile of v1, /device:TPU:0, one launch (start us, length us, event | category | flops | bytes accessed | tf_op | source)
XLA Modules:
  0.0 502.7 jit_solution(15090215140268133995)
XLA Ops:
  0.6 1.2 copy.79
  1.9 5.1 %copy.78 = bf16[1,65,64,512]{3,2,1,0:T(8,128)(2,1)} copy(bf16[1,65,64,512]{3,2,1,0:T(8,128)(2,1)} %param.16) | data formatting | bytes 8519680
  7.0 0.6 broadcast_in_dim.61
  7.7 7.4 %all-to-all-start.1 = ((s32[32,1,1]{2,1,0:T(1,128)}), s32[32,1,1]{2,1,0:T(1,128)S(1)}, u32[]{:S(2)}, u32[]{:S(2)}) async-start(s32[32,1,1]{2,1,0:T(1,128)} %broadcast_in_dim.61), calls=%async_computation.1 | async-start | bytes 32768 | tf_op jit(solution)/shard_map/all_to_all | solution.py:301
  15.7 0.1 fusion.16
  15.9 0.1 select_reduce_fusion
  16.0 0.1 reshape.139
  16.1 2.6 copy.46
  18.7 0.6 pad.4.ids_ref
  19.3 208.7 %exchange.1 = (bf16[32,4,64,512]{3,2,1,0:T(8,128)(2,1)}, bf16[32,4,32,128]{3,2,1,0:T(8,128)(2,1)}, bf16[64,12288]{1,0:T(8,128)(2,1)}) custom-call(s32[32,1,128]{2,1,0:T(1,128)} %pad.4.ids_ref, bf16[64,7168]{1,0:T(8,128)(2,1)} %bitcast.51, bf16[65,64,512]{2,1,0:T(8,128)(2,1)} %bitcast.46, bf16[65,64,64]{2,1,0:T(8,128)(2,1)} %bitcast.52, bf16[7168,12288]{1,0:T(8,128)(2,1)} %w_q.1), custom_call_target="tpu_custom_call" | custom-call | tf_op jit(solution)/shard_map/exchange/pallas_call | solution.py:153
  228.0 0.0 copy-start.7
  228.0 0.0 copy-start.1
  228.0 3.8 reshape.140
  231.9 0.2 slice.54
  232.1 0.0 slice-start.1
  232.1 6.4 %fusion.25 = f32[64,576]{1,0:T(8,128)S(1)} fusion(bf16[7168,576]{0,1:T(8,128)(2,1)} %param.19, bf16[1,64,7168]{2,1,0:T(8,128)(2,1)S(1)} %copy-done.1), kind=kOutput, calls=%fused_computation.53 | convolution fusion | flops 528482304 | bytes 9322496 | tf_op jit(solution)/shard_map/dot_general | solution.py:326
  238.6 0.1 multiply_reduce_fusion
  238.7 0.0 slice-start.2
  238.7 0.6 copy_convert_fusion
  239.3 0.2 subtract_convert_fusion.1
  239.5 0.8 subtract_convert_fusion
  240.3 0.0 slice-start
  240.3 0.6 pad_maximum_fusion
  240.9 1.5 pad_maximum_fusion.1.qk_ref
  242.5 0.6 pad_add_fusion.valid_ref
  243.1 0.7 multiply_convert_fusion.newc_ref
  243.8 0.7 pad_maximum_fusion.3.newk_ref
  244.5 20.6 %fusion.6 = bf16[64,64,512]{2,1,0:T(8,128)(2,1)} fusion(bf16[512,64,128]{2,1,0:T(8,128)(2,1)S(1)} %bitcast.50, bf16[64,64,128]{2,1,0:T(8,128)(2,1)S(1)} %slice-done), kind=kOutput, calls=%fused_computation.8 | convolution fusion | flops 538968064 | bytes 13631488 | tf_op jit(solution)/shard_map/chn,lhn->hcl/dot_general | solution.py:336
  265.1 110.4 %attend.1 = bf16[4096,512]{1,0:T(8,128)(2,1)} custom-call(s32[65]{0:T(128)} %pad_add_fusion.valid_ref, bf16[4096,512]{1,0:T(8,128)(2,1)} %bitcast.47, bf16[4096,128]{1,0:T(8,128)(2,1)} %pad_maximum_fusion.1.qk_ref, bf16[128,64,512]{2,1,0:T(8,128)(2,1)} %bitcast.48, bf16[128,32,128]{2,1,0:T(8,128)(2,1)} %bitcast.55, ...), custom_call_target="tpu_custom_call" | custom-call | tf_op jit(solution)/shard_map/attend/pallas_call | solution.py:271
  375.6 0.0 copy-start.5
  375.6 22.0 %fusion.12 = bf16[64,8,8,128]{3,2,1,0:T(8,128)(2,1)S(1)} fusion(bf16[64,64,512]{2,1,0:T(8,128)(2,1)} %bitcast.54, bf16[512,64,128]{2,1,0:T(8,128)(2,1)} %param.22), kind=kOutput, calls=%fused_computation.12 | convolution fusion | flops 537395200 | bytes 13631488 | tf_op jit(solution)/shard_map/hcl,lhv->chv/dot_general | solution.py:341
  397.6 0.1 pad_maximum_fusion.2
  397.7 0.7 reshape.147
  398.3 0.0 all-to-all-done.1
  398.3 42.9 %all-to-all-start = ((bf16[32,2,576]{2,1,0:T(2,128)(2,1)}), bf16[32,2,576]{2,1,0:T(2,128)(2,1)S(1)}, u32[]{:S(2)}, u32[]{:S(2)}) async-start(bf16[32,2,576]{2,1,0:T(2,128)(2,1)} %reshape.147), calls=%async_computation | async-start | bytes 163840 | tf_op jit(solution)/shard_map/all_to_all | solution.py:302
  441.2 0.7 reduce
  441.9 0.1 select_reduce_fusion.1
  442.0 6.6 %all-to-all-done = bf16[32,2,576]{2,1,0:T(2,128)(2,1)S(1)} async-done(((bf16[32,2,576]{2,1,0:T(2,128)(2,1)}), bf16[32,2,576]{2,1,0:T(2,128)(2,1)S(1)}, u32[]{:S(2)}, u32[]{:S(2)}) %all-to-all-start) | async-done | bytes 73760 | tf_op jit(solution)/shard_map/all_to_all | solution.py:302
  448.6 1.4 gather_fusion
  450.0 2.6 all-to-all-start.2
  452.6 40.1 %fusion.5 = bf16[1,64,7168]{2,1,0:T(8,128)(2,1)} fusion(bf16[8192,7168]{1,0:T(8,128)(2,1)} %param.23, bf16[64,8,8,128]{3,2,1,0:T(8,128)(2,1)S(1)} %fusion.12, bf16[1,64,7168]{2,1,0:T(8,128)(2,1)S(1)} %copy-done.1), kind=kOutput, calls=%fused_computation.7 | convolution fusion | flops 7517569024 | bytes 120324096 | tf_op jit(solution)/shard_map/dot_general | solution.py:342
  492.7 0.0 all-to-all-done.2
  492.7 0.1 reshape.148
  492.7 0.6 fusion.20
  493.4 0.5 copy.52
  493.9 7.6 %dynamic_update_slice.7 = bf16[1,65,64,64]{1,3,2,0:T(8,128)(2,1)S(1)} dynamic-update-slice(bf16[1,65,64,64]{1,3,2,0:T(8,128)(2,1)S(1)} %copy-done.3, bf16[1,1,64,64]{1,3,2,0:T(8,128)(2,1)S(1)} %copy.52, s32[]{:T(128)} %constant.37.clone.1, s32[]{:T(128)} %constant.47.clone.1, s32[]{:T(128)} %constant.37.clone.1, s32[]{:T(128)} %constant.37.clone.1) | dynamic-update-slice | bytes 16388 | tf_op jit(solution)/shard_map/dynamic_update_slice | solution.py:306
  501.5 0.0 copy-start.4
  501.5 1.0 copy-done.4
  (26 shorter events, 0.1 us)
Async XLA Ops:
  1.9 14.2 %copy-start.2 = (bf16[1,65,64,64]{1,3,2,0:T(8,128)(2,1)}, bf16[1,65,64,64]{1,3,2,0:T(8,128)(2,1)S(1)}, u32[]{:S(2)}) copy-start(bf16[1,65,64,64]{1,3,2,0:T(8,128)(2,1)S(1)} %copy.79) | copy-start | bytes 1597444
  1.9 5.2 %copy-start.8 = (s32[1,1,2]{2,1,0:T(1,128)S(1)}, s32[1,1,2]{2,1,0:T(1,128)}, u32[]{:S(2)}) copy-start(s32[1,1,2]{2,1,0:T(1,128)} %param.15) | copy-start | bytes 28
  1.9 13.8 %copy-start.6 = (s32[1,64,2]{1,2,0:T(2,128)S(1)}, s32[1,64,2]{1,2,0:T(2,128)}, u32[]{:S(2)}) copy-start(s32[1,64,2]{1,2,0:T(2,128)} %param.14) | copy-start | bytes 1540
  7.7 390.7 %all-to-all-start.1 = ((s32[32,1,1]{2,1,0:T(1,128)}), s32[32,1,1]{2,1,0:T(1,128)S(1)}, u32[]{:S(2)}, u32[]{:S(2)}) async-start(s32[32,1,1]{2,1,0:T(1,128)} %broadcast_in_dim.61), calls=%async_computation.1 | async-start | bytes 32768 | tf_op jit(solution)/shard_map/all_to_all | solution.py:301
  228.0 4.1 copy-start.7
  228.0 4.1 copy-start.1
  231.8 6.7 %copy-start = (bf16[64,64,192]{2,1,0:T(8,128)(2,1)}, bf16[64,64,192]{2,1,0:T(8,128)(2,1)S(1)}, u32[]{:S(2)}) copy-start(bf16[64,64,192]{2,1,0:T(8,128)(2,1)S(1)} %reshape.140) | copy-start | bytes 4718596
  232.1 12.4 %slice-start.1 = ((s8[8388608]{0:T(1024)(128)(4,1)}), s8[4194304]{0:T(1024)(128)(4,1)S(1)}, s32[]{:S(2)}) async-start(s8[8388608]{0:T(1024)(128)(4,1)} %bitcast.49), calls=%async_computation.4 | async-start | bytes 8388608
  238.7 5.8 %slice-start.2 = ((s8[8388608]{0:T(1024)(128)(4,1)}), s8[4194304]{0:T(1024)(128)(4,1)S(1)}, s32[]{:S(2)}) async-start(s8[8388608]{0:T(1024)(128)(4,1)} %bitcast.49), calls=%async_computation.5 | async-start | bytes 8388608
  240.3 4.2 slice-start
  375.6 22.0 %copy-start.5 = (bf16[64,512]{1,0:T(8,128)(2,1)S(1)}, bf16[64,512]{1,0:T(8,128)(2,1)}, u32[]{:S(2)}) copy-start(bf16[64,512]{1,0:T(8,128)(2,1)} %multiply_convert_fusion.newc_ref) | copy-start | bytes 196612
  398.3 50.3 %all-to-all-start = ((bf16[32,2,576]{2,1,0:T(2,128)(2,1)}), bf16[32,2,576]{2,1,0:T(2,128)(2,1)S(1)}, u32[]{:S(2)}, u32[]{:S(2)}) async-start(bf16[32,2,576]{2,1,0:T(2,128)(2,1)} %reshape.147), calls=%async_computation | async-start | bytes 163840 | tf_op jit(solution)/shard_map/all_to_all | solution.py:302
  450.0 42.7 %all-to-all-start.2 = ((bf16[32,2,576]{2,1,0:T(2,128)(2,1)}), bf16[32,2,576]{2,1,0:T(2,128)(2,1)S(1)}, u32[]{:S(2)}, u32[]{:S(2)}) async-start(bf16[32,2,576]{2,1,0:T(2,128)(2,1)} %gather_fusion), calls=%async_computation.2 | async-start | bytes 163840 | tf_op jit(solution)/shard_map/all_to_all | solution.py:304
  452.5 41.4 %copy-start.3 = (bf16[1,65,64,64]{1,3,2,0:T(8,128)(2,1)S(1)}, bf16[1,65,64,64]{1,3,2,0:T(8,128)(2,1)}, u32[]{:S(2)}) copy-start(bf16[1,65,64,64]{1,3,2,0:T(8,128)(2,1)} %copy-done.2) | copy-start | bytes 1597444
  501.5 1.0 copy-start.4

commit v2 on v0

v2 whole, which is shorter than its diff:
```python
import functools

import jax
import jax.numpy as jnp
from jax import lax
from jax.experimental import pallas as pl
from jax.experimental.pallas import tpu as pltpu
from jax.sharding import PartitionSpec as P

PAGE_LEN = 64
LATENT = 512
ROPE_DIM = 64
NOPE_DIM = 128
VALUE_DIM = 128
HEADS = 64
CHUNK = 64
D_MODEL = 7168
SLOTS = 4
NORM_EPS = 1e-6
ROPE_BASE = 10000.0
MESH = pl.DeviceIdType.MESH
VMEM_LIMIT = 63 * 1024 * 1024
SCALE2 = (NOPE_DIM + ROPE_DIM) ** -0.5 * 1.4426950408889634
ROWS = HEADS * CHUNK
SUB = 256
SUBS = 4
W_BLK = 256
KV_ROWS = 896
H_BLK = 8
LAST_DIMS = (((1,), (1,)), ((), ()))
BF16 = jnp.bfloat16
F32 = jnp.float32


def xor(a, b, bits):
    out = 0
    for i in range(bits):
        w = 2 ** i
        out = out + w * (((a // w) % 2 + (b // w) % 2) % 2)
    return out


def step_code(k):
    return k // 2 + 16 * (k % 2)


def rope(values, cos2, sin2):
    half = ROPE_DIM // 2
    swapped = jnp.concatenate([values[:, half:], values[:, :half]], axis=-1)
    return values * cos2 + swapped * sin2


def layer_kernel(n, ids_ref, x_ref, bias_ref, rot_ref, gain_ref, cache_c, cache_kr, w_q, w_dkv, w_uk, w_uv,
                 o_lat, wuv_out, page_c_out, page_k_out,
                 ids_in, ids_smem, cc, ck, kp, stage_c, stage_k, land_c, land_k, wbuf, q_all, qc, qk, m_ref, l_ref, acc,
                 hbuf, h32, hout, kvbuf, new_c, new_k, kk, part_out, part_mid, part_fwd, part_in, c32,
                 loc_sem, id_send, id_recv, c_send, c_recv, k_send, k_recv, p_send, p_recv, f_send, f_recv, w_sem, h_sem, ho_sem, kv_sem, out_sem):
    me = lax.axis_index("pool")
    bits = n.bit_length() - 1
    pages = kp.shape[0]
    n_blk = w_q.shape[1] // W_BLK
    n_kv = D_MODEL // KV_ROWS
    n_h = HEADS // H_BLK

    load_c = pltpu.make_async_copy(cache_c.at[pl.ds(0, pages)], cc, loc_sem.at[0])
    load_k = pltpu.make_async_copy(cache_kr.at[pl.ds(0, pages)], ck, loc_sem.at[1])
    load_k.start()
    load_c.start()

    def peer_of(k):
        return xor(me, step_code(k), bits)

    barrier = pltpu.get_barrier_semaphore()

    @pl.loop(1, n)
    def _(k):
        pl.semaphore_signal(barrier, inc=1, device_id=(peer_of(k),), device_id_type=MESH)

    def kv_copy(i, slot):
        return pltpu.make_async_copy(w_dkv.at[pl.ds(pl.multiple_of(i * KV_ROWS, KV_ROWS), KV_ROWS)], kvbuf.at[slot], kv_sem.at[slot])

    def w_copy(i, slot):
        return pltpu.make_async_copy(w_q.at[:, pl.ds(pl.multiple_of(i * W_BLK, W_BLK), W_BLK)], wbuf.at[slot], w_sem.at[slot])

    kv_copy(0, 0).start()
    kv_copy(1, 1).start()
    pl.semaphore_wait(barrier, n - 1)

    def id_copy(k):
        peer = peer_of(k)
        return pltpu.make_async_remote_copy(src_ref=ids_ref.at[peer], dst_ref=ids_in.at[k], send_sem=id_send.at[k],
                                            recv_sem=id_recv.at[k], device_id=(peer,), device_id_type=MESH)

    @pl.loop(1, n)
    def _(k):
        id_copy(k).start()

    own_ids = pltpu.make_async_copy(ids_ref.at[me], ids_in.at[0], loc_sem.at[2])
    own_ids.start()
    load_k.wait()

    @pl.loop(0, pages)
    def _(i):
        page = ck[i]
        kp[i] = jnp.concatenate([page[: PAGE_LEN // 2], page[PAGE_LEN // 2:]], axis=-1)

    load_c.wait()
    own_ids.wait()

    @pl.loop(1, n)
    def _(k):
        id_copy(k).wait_recv()

    to_smem = pltpu.make_async_copy(ids_in, ids_smem, loc_sem.at[3])
    to_smem.start()
    to_smem.wait()

    def c_copy(k):
        return pltpu.make_async_remote_copy(src_ref=stage_c.at[k], dst_ref=land_c.at[k], send_sem=c_send.at[k],
                                            recv_sem=c_recv.at[k], device_id=(peer_of(k),), device_id_type=MESH)

    def k_copy(k):
        return pltpu.make_async_remote_copy(src_ref=stage_k.at[k], dst_ref=land_k.at[k], send_sem=k_send.at[k],
                                            recv_sem=k_recv.at[k], device_id=(peer_of(k),), device_id_type=MESH)

    def send_pages(k):
        for s in range(SLOTS):
            page = ids_smem[k, 0, s]
            stage_c[k, s] = cc[page]
            stage_k[k, s] = kp[page]
        c_copy(k).start()
        k_copy(k).start()

    @pl.loop(1, n // 2)
    def _(k):
        send_pages(k)

    w_copy(0, 0).start()
    w_copy(1, 1).start()

    kv = jnp.zeros((CHUNK, LATENT + ROPE_DIM), F32)
    for i in range(n_kv):
        kv_copy(i, i % 2).wait()
        kv = kv + jnp.dot(x_ref[:, i * KV_ROWS:(i + 1) * KV_ROWS], kvbuf[i % 2], preferred_element_type=F32)
        if i + 2 < n_kv:
            kv_copy(i + 2, i % 2).start()
    lat = kv[:, :LATENT]
    inv_rms = lax.rsqrt(jnp.mean(lat * lat, axis=-1, keepdims=True) + NORM_EPS)
    c_new = (lat * inv_rms * gain_ref[...]).astype(BF16)
    cos2 = rot_ref[0]
    sin2 = rot_ref[1]
    kr_new = rope(kv[:, LATENT:], cos2, sin2).astype(BF16)
    new_c[...] = c_new
    new_k[...] = kr_new

    for g in range(LATENT // 128):
        c32[:, g, :] = c_new[:, g * 128:(g + 1) * 128].astype(F32)
    c32[:, 4, :] = jnp.concatenate([kr_new, kr_new], axis=-1).astype(F32)
    low = lax.broadcasted_iota(jnp.int32, (1, 128), 1) < ROPE_DIM
    for i in range(n):
        a = c32[2 * i]
        b = c32[2 * i + 1]
        last = jnp.where(low, a[4:5], b[4:5])
        part_out[i] = jnp.concatenate([a[:4], b[:4], jnp.broadcast_to(last, (8, 128))], axis=0).astype(BF16)

    def p_copy(k):
        peer = peer_of(k)
        return pltpu.make_async_remote_copy(src_ref=part_out.at[peer], dst_ref=part_mid.at[k], send_sem=p_send.at[k],
                                            recv_sem=p_recv.at[k], device_id=(peer,), device_id_type=MESH)

    def f_copy(k):
        peer = peer_of(k)
        return pltpu.make_async_remote_copy(src_ref=part_fwd.at[k], dst_ref=part_in.at[me], send_sem=f_send.at[k],
                                            recv_sem=f_recv.at[k], device_id=(peer,), device_id_type=MESH)

    def f_arrival(k):
        peer = peer_of(k)
        return pltpu.make_async_remote_copy(src_ref=part_fwd.at[k], dst_ref=part_in.at[peer], send_sem=f_send.at[k],
                                            recv_sem=f_recv.at[k], device_id=(peer,), device_id_type=MESH)

    @pl.loop(1, n)
    def _(k):
        p_copy(k).start()

    part_mid[0] = part_out[me]

    @pl.loop(n // 2, n)
    def _(k):
        send_pages(k)

    for s in range(SLOTS):
        page = ids_smem[0, 0, s]
        land_c[0, s] = cc[page]
        land_k[0, s] = kp[page]

    @pl.loop(0, n_blk // 2)
    def _(g):
        for slot in range(2):
            i = g * 2 + slot
            w_copy(i, slot).wait()
            part = jnp.dot(x_ref[...], wbuf[slot], preferred_element_type=F32)
            q_all[:, pl.ds(pl.multiple_of(i * W_BLK, W_BLK), W_BLK)] = part.astype(BF16)

            @pl.when(i + 2 < n_blk)
            def _():
                w_copy(i + 2, slot).start()

    def h_copy(src, i, slot):
        return pltpu.make_async_copy(src.at[:, pl.ds(pl.multiple_of(i * H_BLK, H_BLK), H_BLK)], hbuf.at[slot], h_sem.at[slot])

    h_copy(w_uk, 0, 0).start()

    @pl.loop(0, n_h)
    def _(i):
        slot = i % 2
        h_copy(w_uk, i, slot).wait()

        @pl.when(i + 1 < n_h)
        def _():
            h_copy(w_uk, i + 1, 1 - slot).start()

        h32[...] = hbuf[slot].astype(F32)
        for pair in range(H_BLK // 2):
            q2 = q_all[:, pl.ds(pl.multiple_of((i * (H_BLK // 2) + pair) * 384, 128), 384)]
            q32 = q2.astype(F32)
            for odd in range(2):
                j = pair * 2 + odd
                base = odd * (NOPE_DIM + ROPE_DIM)
                wk = h32[:, j, :].astype(BF16)
                u = lax.dot_general(q2[:, base:base + NOPE_DIM], wk, LAST_DIMS, preferred_element_type=F32)
                qr = rope(q32[:, base + NOPE_DIM:base + NOPE_DIM + ROPE_DIM], cos2, sin2).astype(BF16)
                at = pl.ds(pl.multiple_of((i * H_BLK + j) * CHUNK, CHUNK), CHUNK)
                qc[at, :] = u.astype(BF16)
                qk[at, :] = jnp.concatenate([qr, qr], axis=-1)

    def ho_copy(i):
        return pltpu.make_async_copy(hout, wuv_out.at[pl.ds(pl.multiple_of(i * H_BLK, H_BLK), H_BLK)], ho_sem.at[0])

    h_copy(w_uv, 0, 0).start()

    @pl.loop(0, n_h)
    def _(i):
        slot = i % 2
        h_copy(w_uv, i, slot).wait()

        @pl.when(i + 1 < n_h)
        def _():
            h_copy(w_uv, i + 1, 1 - slot).start()

        h32[...] = hbuf[slot].astype(F32)

        @pl.when(i > 0)
        def _():
            ho_copy(i - 1).wait()

        for j in range(H_BLK):
            hout[j] = h32[:, j, :].astype(BF16)
        ho_copy(i).start()

    def tile(at, s, keys):
        m_old = m_ref[at, :]
        m_new = jnp.maximum(m_old, jnp.max(s, axis=-1, keepdims=True))
        alpha = jnp.exp2(m_old - m_new)
        groups = s.shape[1] // 128
        parts = [jnp.exp2(s[:, g * 128:(g + 1) * 128] - m_new) for g in range(groups)]
        total = parts[0]
        for p in parts[1:]:
            total = total + p
        m_ref[at, :] = m_new
        l_ref[at, :] = l_ref[at, :] * alpha + total
        p = jnp.concatenate([p.astype(BF16) for p in parts], axis=-1)
        pv = jnp.dot(p, keys, preferred_element_type=F32)
        for g in range(LATENT // 128):
            lanes = slice(g * 128, (g + 1) * 128)
            acc[at, lanes] = acc[at, lanes] * alpha + pv[:, lanes]

    first_lanes = lax.broadcasted_iota(jnp.int32, (CHUNK, 2 * ROPE_DIM), 1) < ROPE_DIM

    @pl.loop(0, ROWS // SUB)
    def _(i):
        at = pl.ds(pl.multiple_of(i * SUB, SUB), SUB)
        causal = (lax.broadcasted_iota(jnp.int32, (SUB, CHUNK), 1) <= lax.broadcasted_iota(jnp.int32, (SUB, CHUNK), 0) % CHUNK)
        k64 = jnp.concatenate([new_k[...], jnp.zeros((CHUNK, ROPE_DIM), BF16)], axis=-1)
        s = lax.dot_general(qc[at, :], new_c[...], LAST_DIMS, preferred_element_type=F32)
        s = s + lax.dot_general(qk[at, :], k64, LAST_DIMS, preferred_element_type=F32)
        s = jnp.where(causal, s * SCALE2, -jnp.inf)
        m = jnp.max(s, axis=-1, keepdims=True)
        p = jnp.exp2(s - m)
        m_ref[at, :] = jnp.broadcast_to(m, (SUB, 128))
        l_ref[at, :] = jnp.concatenate([p, jnp.zeros((SUB, 128 - CHUNK), F32)], axis=-1)
        acc[at, :] = jnp.dot(p.astype(BF16), new_c[...], preferred_element_type=F32)

    half_low = lax.broadcasted_iota(jnp.int32, (PAGE_LEN // 2, 2 * ROPE_DIM), 1) < ROPE_DIM

    @pl.loop(0, n // 2)
    def _(t):
        @pl.when(t > 0)
        def _():
            c_copy(2 * t).wait_recv()
            k_copy(2 * t).wait_recv()

        c_copy(2 * t + 1).wait_recv()
        k_copy(2 * t + 1).wait_recv()

        for d in range(2):
            for s in range(SLOTS):
                page = land_k[2 * t + d, s]
                zero = jnp.zeros_like(page)
                base = (d * SLOTS + s) * PAGE_LEN
                kk[base:base + PAGE_LEN // 2, :] = jnp.where(half_low, page, zero)
                kk[base + PAGE_LEN // 2:base + PAGE_LEN, :] = jnp.where(half_low, zero, page)

        @pl.loop(0, ROWS // (SUB * SUBS))
        def _(i):
            keys = land_c[pl.ds(2 * t, 2)].reshape(2 * SLOTS * PAGE_LEN, LATENT)
            bias = bias_ref[t]
            ats = [pl.ds(pl.multiple_of((i * SUBS + u) * SUB, SUB), SUB) for u in range(SUBS)]
            raw = []
            for at in ats:
                s = lax.dot_general(qc[at, :], keys, LAST_DIMS, preferred_element_type=F32)
                raw.append(s + lax.dot_general(qk[at, :], kk[...], LAST_DIMS, preferred_element_type=F32))
            for at, s in zip(ats, raw):
                tile(at, s * SCALE2 + bias, keys)

        @pl.when(t == n // 2 - 6)
        def _():
            @pl.loop(1, n)
            def _(k):
                p_copy(k).wait_recv()

            @pl.loop(0, n)
            def _(k):
                owner = peer_of(k)
                source = jnp.int32(0)
                for j in range(n):
                    source = jnp.where(ids_smem[j, 0, SLOTS] == owner, j, source)
                part_fwd[k] = part_mid[source]

            @pl.loop(1, n)
            def _(k):
                f_copy(k).start()

            part_in[me] = part_fwd[0]

    @pl.loop(0, ROWS // SUB)
    def _(i):
        at = pl.ds(pl.multiple_of(i * SUB, SUB), SUB)
        total = jnp.sum(l_ref[at, :], axis=-1, keepdims=True)
        qc[at, :] = (acc[at, :] / total).astype(BF16)

    out = pltpu.make_async_copy(qc, o_lat, out_sem.at[0])
    out.start()

    @pl.loop(1, n)
    def _(k):
        f_arrival(k).wait_recv()

    for i in range(n):
        part = part_in[i].astype(F32)
        c32[2 * i, 0:4] = part[0:4]
        c32[2 * i + 1, 0:4] = part[4:8]
        c32[2 * i, 4:5] = part[8:9]
        c32[2 * i + 1, 4:5] = jnp.concatenate([part[8:9, ROPE_DIM:], part[8:9, :ROPE_DIM]], axis=-1)
    for g in range(LATENT // 128):
        new_c[:, g * 128:(g + 1) * 128] = c32[:, g, :].astype(BF16)
    new_k[...] = c32[:, 4, :][:, :ROPE_DIM].astype(BF16)
    out_pc = pltpu.make_async_copy(new_c, page_c_out, out_sem.at[1])
    out_pk = pltpu.make_async_copy(new_k, page_k_out, out_sem.at[2])
    out_pc.start()
    out_pk.start()

    @pl.loop(1, n)
    def _(k):
        id_copy(k).wait_send()
        c_copy(k).wait_send()
        k_copy(k).wait_send()
        p_copy(k).wait_send()
        f_copy(k).wait_send()

    ho_copy(n_h - 1).wait()
    out.wait()
    out_pc.wait()
    out_pk.wait()


def layer(n, ids, x, bias, rot, gain, cache_c, cache_kr, w_q, w_dkv, w_uk, w_uv):
    pages = cache_c.shape[0] - 1
    any_spec = pl.BlockSpec(memory_space=pl.ANY)
    vmem = pl.BlockSpec(memory_space=pltpu.VMEM)
    dma = pltpu.SemaphoreType.DMA
    return pl.pallas_call(
        functools.partial(layer_kernel, n),
        name="layer",
        out_shape=(
            jax.ShapeDtypeStruct((ROWS, LATENT), BF16),
            jax.ShapeDtypeStruct((HEADS, LATENT, VALUE_DIM), BF16),
            jax.ShapeDtypeStruct((CHUNK, LATENT), BF16),
            jax.ShapeDtypeStruct((CHUNK, ROPE_DIM), BF16),
        ),
        in_specs=[vmem] * 5 + [any_spec] * 6,
        out_specs=(any_spec,) * 4,
        scratch_shapes=[
            pltpu.VMEM((n, 1, 128), jnp.int32),
            pltpu.SMEM((n, 1, 128), jnp.int32),
            pltpu.VMEM((pages, PAGE_LEN, LATENT), BF16),
            pltpu.VMEM((pages, PAGE_LEN, ROPE_DIM), BF16),
            pltpu.VMEM((pages, PAGE_LEN // 2, 2 * ROPE_DIM), BF16),
            pltpu.VMEM((n, SLOTS, PAGE_LEN, LATENT), BF16),
            pltpu.VMEM((n, SLOTS, PAGE_LEN // 2, 2 * ROPE_DIM), BF16),
            pltpu.VMEM((n, SLOTS, PAGE_LEN, LATENT), BF16),
            pltpu.VMEM((n, SLOTS, PAGE_LEN // 2, 2 * ROPE_DIM), BF16),
            pltpu.VMEM((2, D_MODEL, W_BLK), BF16),
            pltpu.VMEM((CHUNK, HEADS * (NOPE_DIM + ROPE_DIM)), BF16),
            pltpu.VMEM((ROWS, LATENT), BF16),
            pltpu.VMEM((ROWS, 2 * ROPE_DIM), BF16),
            pltpu.VMEM((ROWS, 128), F32),
            pltpu.VMEM((ROWS, 128), F32),
            pltpu.VMEM((ROWS, LATENT), F32),
            pltpu.VMEM((2, LATENT, H_BLK, NOPE_DIM), BF16),
            pltpu.VMEM((LATENT, H_BLK, NOPE_DIM), F32),
            pltpu.VMEM((H_BLK, LATENT, VALUE_DIM), BF16),
            pltpu.VMEM((2, KV_ROWS, LATENT + ROPE_DIM), BF16),
            pltpu.VMEM((CHUNK, LATENT), BF16),
            pltpu.VMEM((CHUNK, ROPE_DIM), BF16),
            pltpu.VMEM((2 * SLOTS * PAGE_LEN, 2 * ROPE_DIM), BF16),
            pltpu.VMEM((n, 16, 128), BF16),
            pltpu.VMEM((n, 16, 128), BF16),
            pltpu.VMEM((n, 16, 128), BF16),
            pltpu.VMEM((n, 16, 128), BF16),
            pltpu.VMEM((CHUNK, 8, 128), F32),
            dma((4,)),
        ] + [dma((n,))] * 10 + [dma((2,)), dma((2,)), dma((1,)), dma((2,)), dma((3,))],
        compiler_params=pltpu.CompilerParams(collective_id=0, has_side_effects=True, vmem_limit_bytes=VMEM_LIMIT),
    )(ids, x, bias, rot, gain, cache_c, cache_kr, w_q, w_dkv, w_uk, w_uv)


O_BLK = 256
O_BUFS = 6


def finish_kernel(x_ref, o_lat, wuv, w_o, cache_c, cache_kr, page_c, page_k, y_ref, out_c, out_kr,
                  lat, wv, heads, wbuf, cbuf, kbuf, lat_sem, wv_sem, w_sem, in_sem, out_sem):
    n_blk = w_o.shape[1] // O_BLK
    n_h = HEADS // H_BLK
    pages = cache_c.shape[0] - 1

    def lat_copy(i):
        at = pl.ds(pl.multiple_of(i * H_BLK * CHUNK, 8), H_BLK * CHUNK)
        return pltpu.make_async_copy(o_lat.at[at], lat.at[at], lat_sem.at[i])

    def wv_copy(i):
        at = pl.ds(pl.multiple_of(i * H_BLK, H_BLK), H_BLK)
        return pltpu.make_async_copy(wuv.at[at], wv.at[at], wv_sem.at[i])

    def w_copy(i, slot):
        return pltpu.make_async_copy(w_o.at[:, pl.ds(pl.multiple_of(i * O_BLK, O_BLK), O_BLK)], wbuf.at[slot], w_sem.at[slot])

    for i in range(n_h):
        lat_copy(i).start()
        wv_copy(i).start()
    ins = [pltpu.make_async_copy(cache_c.at[pl.ds(0, pages)], cbuf.at[pl.ds(0, pages)], in_sem.at[0]),
           pltpu.make_async_copy(cache_kr.at[pl.ds(0, pages)], kbuf.at[pl.ds(0, pages)], in_sem.at[1]),
           pltpu.make_async_copy(page_c, cbuf.at[pages], in_sem.at[2]),
           pltpu.make_async_copy(page_k, kbuf.at[pages], in_sem.at[3])]
    for i in range(O_BUFS):
        w_copy(i, i).start()
    for c in ins:
        c.start()

    @pl.loop(0, n_h)
    def _(i):
        lat_copy(i).wait()
        wv_copy(i).wait()
        for j in range(H_BLK):
            h = i * H_BLK + j
            o = jnp.dot(lat[pl.ds(pl.multiple_of(h * CHUNK, CHUNK), CHUNK), :], wv[h], preferred_element_type=F32)
            heads[:, pl.ds(pl.multiple_of(h * VALUE_DIM, VALUE_DIM), VALUE_DIM)] = o.astype(BF16)

    for c in ins:
        c.wait()
    outs = [pltpu.make_async_copy(cbuf, out_c, out_sem.at[0]), pltpu.make_async_copy(kbuf, out_kr, out_sem.at[1])]
    for c in outs:
        c.start()

    @pl.loop(0, n_blk)
    def _(i):
        slot = lax.rem(i, O_BUFS)
        w_copy(i, slot).wait()
        at = pl.ds(pl.multiple_of(i * O_BLK, O_BLK), O_BLK)
        part = jnp.dot(heads[...], wbuf[slot], preferred_element_type=F32)
        y_ref[:, at] = (x_ref[:, at].astype(F32) + part).astype(BF16)

        @pl.when(i + O_BUFS < n_blk)
        def _():
            w_copy(i + O_BUFS, slot).start()

    for c in outs:
        c.wait()


def finish(x, o_lat, wuv, w_o, cache_c, cache_kr, page_c, page_k):
    any_spec = pl.BlockSpec(memory_space=pl.ANY)
    vmem = pl.BlockSpec(memory_space=pltpu.VMEM)
    dma = pltpu.SemaphoreType.DMA
    n_h = HEADS // H_BLK
    return pl.pallas_call(
        finish_kernel,
        name="finish",
        out_shape=(
            jax.ShapeDtypeStruct(x.shape, BF16),
            jax.ShapeDtypeStruct(cache_c.shape, BF16),
            jax.ShapeDtypeStruct(cache_kr.shape, BF16),
        ),
        in_specs=[vmem] + [any_spec] * 7,
        out_specs=(vmem, any_spec, any_spec),
        scratch_shapes=[
            pltpu.VMEM(o_lat.shape, BF16),
            pltpu.VMEM(wuv.shape, BF16),
            pltpu.VMEM((CHUNK, HEADS * VALUE_DIM), BF16),
            pltpu.VMEM((O_BUFS, HEADS * VALUE_DIM, O_BLK), BF16),
            pltpu.VMEM(cache_c.shape, BF16),
            pltpu.VMEM(cache_kr.shape, BF16),
            dma((n_h,)),
            dma((n_h,)),
            dma((O_BUFS,)),
            dma((4,)),
            dma((2,)),
        ],
        compiler_params=pltpu.CompilerParams(vmem_limit_bytes=VMEM_LIMIT),
    )(x, o_lat, wuv, w_o, cache_c, cache_kr, page_c, page_k)


def solution(mesh):
    n = mesh.shape["pool"]

    def device_step(hidden, pre_len, pre_table, wr_table, cache_c, cache_kr, w_q, w_dkv, g_kv, w_uk, w_uv, w_o):
        x = hidden[0]
        me = lax.axis_index("pool")
        owners = pre_table[0, :, 0]
        table_pages = owners.shape[0]
        earlier = jnp.arange(table_pages)[:, None] > jnp.arange(table_pages)[None, :]
        rank = jnp.sum(jnp.where(earlier & (owners[:, None] == owners[None, :]), 1, 0), axis=1)
        pos = jnp.where(owners >= 0, owners * SLOTS + rank, -1)
        lanes = jnp.arange(128, dtype=jnp.int32)
        slot_of = jnp.where(lanes < SLOTS, jnp.arange(n, dtype=jnp.int32)[:, None] * SLOTS + lanes, -2)
        asked = jnp.sum(jnp.where(pos[None, None, :] == slot_of[:, :, None], pre_table[0, :, 1], 0), axis=2)
        ids = jnp.where(lanes == SLOTS, wr_table[0, 0, 0], asked)[:, None, :].astype(jnp.int32)
        keys = jnp.arange(2 * SLOTS * PAGE_LEN, dtype=jnp.int32)
        owner_of = jnp.bitwise_xor(me, jnp.arange(n // 2, dtype=jnp.int32)[:, None] + 16 * (keys // (SLOTS * PAGE_LEN)))
        counts = jnp.sum(jnp.where(owner_of[:, :: SLOTS * PAGE_LEN, None] == owners, 1, 0), axis=2)
        counts = jnp.repeat(counts, SLOTS * PAGE_LEN, axis=1)
        bias = jnp.where((keys // PAGE_LEN) % SLOTS < counts, 0.0, -jnp.inf).astype(F32)[:, None, :]
        cos_tab, sin_tab = rope_tables(pre_len[0] + jnp.arange(CHUNK))
        rot = jnp.stack([jnp.concatenate([cos_tab, cos_tab], -1), jnp.concatenate([-sin_tab, sin_tab], -1)])
        o_lat, wuv, page_c, page_k = layer(n, ids, x, bias, rot, g_kv.astype(F32)[None], cache_c[0], cache_kr[0], w_q, w_dkv, w_uk, w_uv)
        y, out_c, out_kr = finish(x, o_lat, wuv, w_o, cache_c[0], cache_kr[0], page_c, page_k)
        return y[None], out_c[None], out_kr[None]

    row_spec = P("pool")
    rep_spec = P()
    return jax.shard_map(device_step, mesh=mesh, in_specs=(row_spec,) * 6 + (rep_spec,) * 6, out_specs=(row_spec,) * 3, check_vma=False)


def rope_tables(positions):
    half_dim = ROPE_DIM // 2
    inv_freq = ROPE_BASE ** (-jnp.arange(half_dim, dtype=F32) / half_dim)
    angles = positions.astype(F32)[..., None] * inv_freq
    return jnp.cos(angles), jnp.sin(angles)
```

time: 516 us -> 348 us (0.67)
  the two profiles are of different devices: /device:TPU:3 before, /device:TPU:0 now
where the time goes in v2:
time: 348 us; the launch traced here: 346 us
  Pallas kernels  319 us (92%)
  local copies, waits for them, and re-layouts  20 us (6%)
  other arithmetic  5.56 us (2%)
    pallas_call x1, Pallas kernels, layer(): pl.pallas_call(functools.partial(layer_kernel, n), name='layer', out_shap...  273 us
    pallas_call x1, Pallas kernels, finish(): pl.pallas_call(finish_kernel, name='finish', out_shape=(jax.ShapeDtypeStr...  46.3 us
    unnamed x3, local copies, waits for them, and re-layouts  19 us

profile of v2, /device:TPU:0, one launch (start us, length us, event | category | flops | bytes accessed | tf_op | source)
XLA Modules:
  0.0 346.3 jit_solution(18301823684650326425)
XLA Ops:
  1.3 0.8 slice_bitcast_fusion.1
  2.1 0.2 select_reduce_fusion.1
  2.3 0.7 compare_select_fusion.1
  3.0 1.3 broadcast_in_dim.102
  4.2 0.1 add_select_fusion
  4.3 0.2 select_reduce_fusion
  4.5 1.3 broadcast_select_fusion.ids_ref
  5.8 0.2 multiply_cosine_fusion
  6.0 0.1 maximum_bitcast_fusion
  6.1 0.6 pad_maximum_fusion.rot_ref
  6.7 0.1 add_xor_fusion
  6.9 0.2 select_reduce_fusion.2
  7.0 0.1 copy.18
  7.1 0.1 broadcast_in_dim.94
  7.2 0.1 reshape.162
  7.3 0.6 compare_select_fusion.bias_ref
  7.9 3.5 %copy.19 = bf16[1,65,64,64]{3,2,1,0:T(8,128)(2,1)} copy(bf16[1,65,64,64]{1,3,2,0:T(8,128)(2,1)} %param.17) | data formatting | bytes 1064960 | tf_op args[5]
  11.5 12.4 %copy.20.w_dkv = bf16[7168,576]{1,0:T(8,128)(2,1)} copy(bf16[7168,576]{0,1:T(8,128)(2,1)} %param.19) | data formatting | bytes 16515072 | tf_op args[7]
  23.9 273.0 %layer.1 = (bf16[4096,512]{1,0:T(8,128)(2,1)}, bf16[64,512,128]{2,1,0:T(8,128)(2,1)}, bf16[64,512]{1,0:T(8,128)(2,1)}, bf16[64,64]{1,0:T(8,128)(2,1)}) custom-call(s32[32,1,128]{2,1,0:T(1,128)} %broadcast_select_fusion.ids_ref, bf16[64,7168]{1,0:T(8,128)(2,1)} %bitcast.26, f32[16,1,512]{2,1,0:T(1,128)} %compare_select_fusion.bias_ref, ...), custom_call_target="tpu_custom_call" | custom-call | tf_op jit(solution)/shard_map/layer/pallas_call | solution.py:391
  296.9 46.3 %finish.1 = (bf16[64,7168]{1,0:T(8,128)(2,1)}, bf16[65,64,512]{2,1,0:T(8,128)(2,1)}, bf16[65,64,64]{2,1,0:T(8,128)(2,1)}) custom-call(bf16[64,7168]{1,0:T(8,128)(2,1)} %bitcast.27, bf16[4096,512]{1,0:T(8,128)(2,1)} %get-tuple-element.10.o_lat, bf16[64,512,128]{2,1,0:T(8,128)(2,1)} %get-tuple-element.11.wuv, bf16[8192,7168]{1,0:T(8,128)(2,1)} %w_o.1, ...), custom_call_target="tpu_custom_call" | custom-call | tf_op jit(solution)/shard_map/finish/pallas_call | solution.py:506
  343.2 3.1 copy.21
  (8 shorter events, 0.1 us)

commit v3 on v2

--- a/solution.py
+++ b/solution.py
@@ -24,7 +24,9 @@
 ROWS = HEADS * CHUNK
 SUB = 256
 SUBS = 4
-W_BLK = 256
+W_BLK = 512
+W_ROWS = 1792
+W_BUFS = 4
 KV_ROWS = 896
 H_BLK = 8
 LAST_DIMS = (((1,), (1,)), ((), ()))
@@ -32,16 +34,19 @@
 F32 = jnp.float32
 
 
-def xor(a, b, bits):
-    out = 0
-    for i in range(bits):
-        w = 2 ** i
-        out = out + w * (((a // w) % 2 + (b // w) % 2) % 2)
+def step_code(k):
+    return lax.div(k, 2) + 16 * lax.rem(k, 2)
+
+
+def flip_weights(me, bits):
+    return [2 ** i - 2 ** (i + 1) * lax.rem(lax.div(me, 2 ** i), 2) for i in range(bits)]
+
+
+def flipped(me, flips, code):
+    out = me
+    for i, f in enumerate(flips):
+        out = out + f * lax.rem(lax.div(code, 2 ** i), 2)
     return out
-
-
-def step_code(k):
-    return k // 2 + 16 * (k % 2)
 
 
 def rope(values, cos2, sin2):
@@ -67,8 +72,11 @@
     load_k.start()
     load_c.start()
 
+    flips = flip_weights(me, bits)
+    any_peer = lax.rem(me + 1, n)
+
     def peer_of(k):
-        return xor(me, step_code(k), bits)
+        return flipped(me, flips, step_code(k))
 
     barrier = pltpu.get_barrier_semaphore()
 
@@ -77,23 +85,25 @@
         pl.semaphore_signal(barrier, inc=1, device_id=(peer_of(k),), device_id_type=MESH)
 
     def kv_copy(i, slot):
-        return pltpu.make_async_copy(w_dkv.at[pl.ds(pl.multiple_of(i * KV_ROWS, KV_ROWS), KV_ROWS)], kvbuf.at[slot], kv_sem.at[slot])
-
-    def w_copy(i, slot):
-        return pltpu.make_async_copy(w_q.at[:, pl.ds(pl.multiple_of(i * W_BLK, W_BLK), W_BLK)], wbuf.at[slot], w_sem.at[slot])
+        return pltpu.make_async_copy(w_dkv.at[:, pl.ds(i * KV_ROWS, KV_ROWS)], kvbuf.at[slot], kv_sem.at[slot])
+
+    n_row = D_MODEL // W_ROWS
+
+    def w_copy(col, r):
+        rows = pl.ds(r * W_ROWS, W_ROWS)
+        return pltpu.make_async_copy(w_q.at[rows, pl.ds(pl.multiple_of(col * W_BLK, W_BLK), W_BLK)], wbuf.at[r], w_sem.at[r])
 
     kv_copy(0, 0).start()
     kv_copy(1, 1).start()
     pl.semaphore_wait(barrier, n - 1)
 
-    def id_copy(k):
-        peer = peer_of(k)
+    def id_copy(k, peer):
         return pltpu.make_async_remote_copy(src_ref=ids_ref.at[peer], dst_ref=ids_in.at[k], send_sem=id_send.at[k],
                                             recv_sem=id_recv.at[k], device_id=(peer,), device_id_type=MESH)
 
     @pl.loop(1, n)
     def _(k):
-        id_copy(k).start()
+        id_copy(k, peer_of(k)).start()
 
     own_ids = pltpu.make_async_copy(ids_ref.at[me], ids_in.at[0], loc_sem.at[2])
     own_ids.start()
@@ -109,39 +119,40 @@
 
     @pl.loop(1, n)
     def _(k):
-        id_copy(k).wait_recv()
+        id_copy(k, any_peer).wait_recv()
 
     to_smem = pltpu.make_async_copy(ids_in, ids_smem, loc_sem.at[3])
     to_smem.start()
     to_smem.wait()
 
-    def c_copy(k):
+    def c_copy(k, peer):
         return pltpu.make_async_remote_copy(src_ref=stage_c.at[k], dst_ref=land_c.at[k], send_sem=c_send.at[k],
-                                            recv_sem=c_recv.at[k], device_id=(peer_of(k),), device_id_type=MESH)
-
-    def k_copy(k):
+                                            recv_sem=c_recv.at[k], device_id=(peer,), device_id_type=MESH)
+
+    def k_copy(k, peer):
         return pltpu.make_async_remote_copy(src_ref=stage_k.at[k], dst_ref=land_k.at[k], send_sem=k_send.at[k],
-                                            recv_sem=k_recv.at[k], device_id=(peer_of(k),), device_id_type=MESH)
+                                            recv_sem=k_recv.at[k], device_id=(peer,), device_id_type=MESH)
 
     def send_pages(k):
+        peer = peer_of(k)
         for s in range(SLOTS):
             page = ids_smem[k, 0, s]
             stage_c[k, s] = cc[page]
             stage_k[k, s] = kp[page]
-        c_copy(k).start()
-        k_copy(k).start()
+        c_copy(k, peer).start()
+        k_copy(k, peer).start()
 
     @pl.loop(1, n // 2)
     def _(k):
         send_pages(k)
 
-    w_copy(0, 0).start()
-    w_copy(1, 1).start()
+    for r in range(n_row):
+        w_copy(0, r).start()
 
     kv = jnp.zeros((CHUNK, LATENT + ROPE_DIM), F32)
     for i in range(n_kv):
         kv_copy(i, i % 2).wait()
-        kv = kv + jnp.dot(x_ref[:, i * KV_ROWS:(i + 1) * KV_ROWS], kvbuf[i % 2], preferred_element_type=F32)
+        kv = kv + lax.dot_general(x_ref[:, i * KV_ROWS:(i + 1) * KV_ROWS], kvbuf[i % 2], LAST_DIMS, preferred_element_type=F32)
         if i + 2 < n_kv:
             kv_copy(i + 2, i % 2).start()
     lat = kv[:, :LATENT]
@@ -163,24 +174,17 @@
         last = jnp.where(low, a[4:5], b[4:5])
         part_out[i] = jnp.concatenate([a[:4], b[:4], jnp.broadcast_to(last, (8, 128))], axis=0).astype(BF16)
 
-    def p_copy(k):
-        peer = peer_of(k)
+    def p_copy(k, peer):
         return pltpu.make_async_remote_copy(src_ref=part_out.at[peer], dst_ref=part_mid.at[k], send_sem=p_send.at[k],
                                             recv_sem=p_recv.at[k], device_id=(peer,), device_id_type=MESH)
 
-    def f_copy(k):
-        peer = peer_of(k)
+    def f_copy(k, peer):
         return pltpu.make_async_remote_copy(src_ref=part_fwd.at[k], dst_ref=part_in.at[me], send_sem=f_send.at[k],
                                             recv_sem=f_recv.at[k], device_id=(peer,), device_id_type=MESH)
 
-    def f_arrival(k):
-        peer = peer_of(k)
-        return pltpu.make_async_remote_copy(src_ref=part_fwd.at[k], dst_ref=part_in.at[peer], send_sem=f_send.at[k],
-                                            recv_sem=f_recv.at[k], device_id=(peer,), device_id_type=MESH)
-
     @pl.loop(1, n)
     def _(k):
-        p_copy(k).start()
+        p_copy(k, peer_of(k)).start()
 
     part_mid[0] = part_out[me]
 
@@ -193,17 +197,18 @@
         land_c[0, s] = cc[page]
         land_k[0, s] = kp[page]
 
-    @pl.loop(0, n_blk // 2)
-    def _(g):
-        for slot in range(2):
-            i = g * 2 + slot
-            w_copy(i, slot).wait()
-            part = jnp.dot(x_ref[...], wbuf[slot], preferred_element_type=F32)
-            q_all[:, pl.ds(pl.multiple_of(i * W_BLK, W_BLK), W_BLK)] = part.astype(BF16)
-
-            @pl.when(i + 2 < n_blk)
+    @pl.loop(0, n_blk)
+    def _(col):
+        total = jnp.zeros((CHUNK, W_BLK), F32)
+        for r in range(n_row):
+            w_copy(col, r).wait()
+            total = total + jnp.dot(x_ref[:, r * W_ROWS:(r + 1) * W_ROWS], wbuf[r], preferred_element_type=F32)
+
+            @pl.when(col + 1 < n_blk)
             def _():
-                w_copy(i + 2, slot).start()
+                w_copy(col + 1, r).start()
+
+        q_all[:, pl.ds(pl.multiple_of(col * W_BLK, W_BLK), W_BLK)] = total.astype(BF16)
 
     def h_copy(src, i, slot):
         return pltpu.make_async_copy(src.at[:, pl.ds(pl.multiple_of(i * H_BLK, H_BLK), H_BLK)], hbuf.at[slot], h_sem.at[slot])
@@ -276,19 +281,22 @@
 
     first_lanes = lax.broadcasted_iota(jnp.int32, (CHUNK, 2 * ROPE_DIM), 1) < ROPE_DIM
 
-    @pl.loop(0, ROWS // SUB)
-    def _(i):
-        at = pl.ds(pl.multiple_of(i * SUB, SUB), SUB)
+    @pl.loop(0, ROWS // (SUB * SUBS))
+    def _(i):
         causal = (lax.broadcasted_iota(jnp.int32, (SUB, CHUNK), 1) <= lax.broadcasted_iota(jnp.int32, (SUB, CHUNK), 0) % CHUNK)
         k64 = jnp.concatenate([new_k[...], jnp.zeros((CHUNK, ROPE_DIM), BF16)], axis=-1)
-        s = lax.dot_general(qc[at, :], new_c[...], LAST_DIMS, preferred_element_type=F32)
-        s = s + lax.dot_general(qk[at, :], k64, LAST_DIMS, preferred_element_type=F32)
-        s = jnp.where(causal, s * SCALE2, -jnp.inf)
-        m = jnp.max(s, axis=-1, keepdims=True)
-        p = jnp.exp2(s - m)
-        m_ref[at, :] = jnp.broadcast_to(m, (SUB, 128))
-        l_ref[at, :] = jnp.concatenate([p, jnp.zeros((SUB, 128 - CHUNK), F32)], axis=-1)
-        acc[at, :] = jnp.dot(p.astype(BF16), new_c[...], preferred_element_type=F32)
+        ats = [pl.ds(pl.multiple_of((i * SUBS + u) * SUB, SUB), SUB) for u in range(SUBS)]
+        raw = []
+        for at in ats:
+            s = lax.dot_general(qc[at, :], new_c[...], LAST_DIMS, preferred_element_type=F32)
+            raw.append(s + lax.dot_general(qk[at, :], k64, LAST_DIMS, preferred_element_type=F32))
+        for at, s in zip(ats, raw):
+            s = jnp.where(causal, s * SCALE2, -jnp.inf)
+            m = jnp.max(s, axis=-1, keepdims=True)
+            p = jnp.exp2(s - m)
+            m_ref[at, :] = jnp.broadcast_to(m, (SUB, 128))
+            l_ref[at, :] = jnp.concatenate([p, jnp.zeros((SUB, 128 - CHUNK), F32)], axis=-1)
+            acc[at, :] = jnp.dot(p.astype(BF16), new_c[...], preferred_element_type=F32)
 
     half_low = lax.broadcasted_iota(jnp.int32, (PAGE_LEN // 2, 2 * ROPE_DIM), 1) < ROPE_DIM
 
@@ -296,11 +304,11 @@
     def _(t):
         @pl.when(t > 0)
         def _():
-            c_copy(2 * t).wait_recv()
-            k_copy(2 * t).wait_recv()
-
-        c_copy(2 * t + 1).wait_recv()
-        k_copy(2 * t + 1).wait_recv()
+            c_copy(2 * t, any_peer).wait_recv()
+            k_copy(2 * t, any_peer).wait_recv()
+
+        c_copy(2 * t + 1, any_peer).wait_recv()
+        k_copy(2 * t + 1, any_peer).wait_recv()
 
         for d in range(2):
             for s in range(SLOTS):
@@ -326,7 +334,7 @@
         def _():
             @pl.loop(1, n)
             def _(k):
-                p_copy(k).wait_recv()
+                p_copy(k, any_peer).wait_recv()
 
             @pl.loop(0, n)
             def _(k):
@@ -338,22 +346,22 @@
 
             @pl.loop(1, n)
             def _(k):
-                f_copy(k).start()
+                f_copy(k, peer_of(k)).start()
 
             part_in[me] = part_fwd[0]
 
     @pl.loop(0, ROWS // SUB)
     def _(i):
         at = pl.ds(pl.multiple_of(i * SUB, SUB), SUB)
-        total = jnp.sum(l_ref[at, :], axis=-1, keepdims=True)
-        qc[at, :] = (acc[at, :] / total).astype(BF16)
+        share = 1.0 / jnp.sum(l_ref[at, :], axis=-1, keepdims=True)
+        qc[at, :] = (acc[at, :] * share).astype(BF16)
 
     out = pltpu.make_async_copy(qc, o_lat, out_sem.at[0])
     out.start()
 
     @pl.loop(1, n)
     def _(k):
-        f_arrival(k).wait_recv()
+        f_copy(k, any_peer).wait_recv()
 
     for i in range(n):
         part = part_in[i].astype(F32)
@@ -371,11 +379,11 @@
 
     @pl.loop(1, n)
     def _(k):
-        id_copy(k).wait_send()
-        c_copy(k).wait_send()
-        k_copy(k).wait_send()
-        p_copy(k).wait_send()
-        f_copy(k).wait_send()
+        id_copy(k, any_peer).wait_send()
+        c_copy(k, any_peer).wait_send()
+        k_copy(k, any_peer).wait_send()
+        p_copy(k, any_peer).wait_send()
+        f_copy(k, any_peer).wait_send()
 
     ho_copy(n_h - 1).wait()
     out.wait()
@@ -409,7 +417,7 @@
             pltpu.VMEM((n, SLOTS, PAGE_LEN // 2, 2 * ROPE_DIM), BF16),
             pltpu.VMEM((n, SLOTS, PAGE_LEN, LATENT), BF16),
             pltpu.VMEM((n, SLOTS, PAGE_LEN // 2, 2 * ROPE_DIM), BF16),
-            pltpu.VMEM((2, D_MODEL, W_BLK), BF16),
+            pltpu.VMEM((W_BUFS, W_ROWS, W_BLK), BF16),
             pltpu.VMEM((CHUNK, HEADS * (NOPE_DIM + ROPE_DIM)), BF16),
             pltpu.VMEM((ROWS, LATENT), BF16),
             pltpu.VMEM((ROWS, 2 * ROPE_DIM), BF16),
@@ -419,7 +427,7 @@
             pltpu.VMEM((2, LATENT, H_BLK, NOPE_DIM), BF16),
             pltpu.VMEM((LATENT, H_BLK, NOPE_DIM), F32),
             pltpu.VMEM((H_BLK, LATENT, VALUE_DIM), BF16),
-            pltpu.VMEM((2, KV_ROWS, LATENT + ROPE_DIM), BF16),
+            pltpu.VMEM((2, LATENT + ROPE_DIM, KV_ROWS), BF16),
             pltpu.VMEM((CHUNK, LATENT), BF16),
             pltpu.VMEM((CHUNK, ROPE_DIM), BF16),
             pltpu.VMEM((2 * SLOTS * PAGE_LEN, 2 * ROPE_DIM), BF16),
@@ -429,7 +437,7 @@
             pltpu.VMEM((n, 16, 128), BF16),
             pltpu.VMEM((CHUNK, 8, 128), F32),
             dma((4,)),
-        ] + [dma((n,))] * 10 + [dma((2,)), dma((2,)), dma((1,)), dma((2,)), dma((3,))],
+        ] + [dma((n,))] * 10 + [dma((W_BUFS,)), dma((2,)), dma((1,)), dma((2,)), dma((3,))],
         compiler_params=pltpu.CompilerParams(collective_id=0, has_side_effects=True, vmem_limit_bytes=VMEM_LIMIT),
     )(ids, x, bias, rot, gain, cache_c, cache_kr, w_q, w_dkv, w_uk, w_uv)
 
@@ -552,7 +560,7 @@
         bias = jnp.where((keys // PAGE_LEN) % SLOTS < counts, 0.0, -jnp.inf).astype(F32)[:, None, :]
         cos_tab, sin_tab = rope_tables(pre_len[0] + jnp.arange(CHUNK))
         rot = jnp.stack([jnp.concatenate([cos_tab, cos_tab], -1), jnp.concatenate([-sin_tab, sin_tab], -1)])
-        o_lat, wuv, page_c, page_k = layer(n, ids, x, bias, rot, g_kv.astype(F32)[None], cache_c[0], cache_kr[0], w_q, w_dkv, w_uk, w_uv)
+        o_lat, wuv, page_c, page_k = layer(n, ids, x, bias, rot, g_kv.astype(F32)[None], cache_c[0], cache_kr[0], w_q, w_dkv.T, w_uk, w_uv)
         y, out_c, out_kr = finish(x, o_lat, wuv, w_o, cache_c[0], cache_kr[0], page_c, page_k)
         return y[None], out_c[None], out_kr[None]
 

time: 348 us -> 307 us (0.88)
  the two profiles are of different devices: /device:TPU:0 before, /device:TPU:8 now
where the time goes in v3:
time: 307 us; the launch traced here: 306 us
  Pallas kernels  292 us (95%)
  local copies, waits for them, and re-layouts  7.62 us (2%)
  other arithmetic  5.57 us (2%)
    pallas_call x1, Pallas kernels, layer(): pl.pallas_call(functools.partial(layer_kernel, n), name='layer', out_shap...  245 us
    pallas_call x1, Pallas kernels, finish(): pl.pallas_call(finish_kernel, name='finish', out_shape=(jax.ShapeDtypeStr...  46.2 us
    unnamed x2, local copies, waits for them, and re-layouts  6.62 us

profile of v3, /device:TPU:8, one launch (start us, length us, event | category | flops | bytes accessed | tf_op | source)
XLA Modules:
  0.0 306.1 jit_solution(11858753924012621519)
XLA Ops:
  1.3 0.8 slice_bitcast_fusion.1
  2.1 0.2 select_reduce_fusion.1
  2.3 0.7 compare_select_fusion.1
  3.0 1.3 broadcast_in_dim.102
  4.2 0.1 add_select_fusion
  4.3 0.2 select_reduce_fusion
  4.5 1.3 broadcast_select_fusion.ids_ref
  5.8 0.2 multiply_cosine_fusion
  6.0 0.1 maximum_bitcast_fusion
  6.1 0.6 pad_maximum_fusion.rot_ref
  6.7 0.1 add_xor_fusion
  6.9 0.2 select_reduce_fusion.2
  7.0 0.1 copy.17
  7.1 0.1 broadcast_in_dim.94
  7.2 0.1 reshape.162
  7.3 0.6 compare_select_fusion.bias_ref
  7.9 3.6 %copy.18 = bf16[1,65,64,64]{3,2,1,0:T(8,128)(2,1)} copy(bf16[1,65,64,64]{1,3,2,0:T(8,128)(2,1)} %param.17) | data formatting | bytes 1064960 | tf_op args[5]
  11.5 245.4 %layer.1 = (bf16[4096,512]{1,0:T(8,128)(2,1)}, bf16[64,512,128]{2,1,0:T(8,128)(2,1)}, bf16[64,512]{1,0:T(8,128)(2,1)}, bf16[64,64]{1,0:T(8,128)(2,1)}) custom-call(s32[32,1,128]{2,1,0:T(1,128)} %broadcast_select_fusion.ids_ref, bf16[64,7168]{1,0:T(8,128)(2,1)} %bitcast.28, f32[16,1,512]{2,1,0:T(1,128)} %compare_select_fusion.bias_ref, ...), custom_call_target="tpu_custom_call" | custom-call | tf_op jit(solution)/shard_map/layer/pallas_call | solution.py:399
  256.8 46.2 %finish.1 = (bf16[64,7168]{1,0:T(8,128)(2,1)}, bf16[65,64,512]{2,1,0:T(8,128)(2,1)}, bf16[65,64,64]{2,1,0:T(8,128)(2,1)}) custom-call(bf16[64,7168]{1,0:T(8,128)(2,1)} %bitcast.29, bf16[4096,512]{1,0:T(8,128)(2,1)} %get-tuple-element.10.o_lat, bf16[64,512,128]{2,1,0:T(8,128)(2,1)} %get-tuple-element.11.wuv, bf16[8192,7168]{1,0:T(8,128)(2,1)} %w_o.1, ...), custom_call_target="tpu_custom_call" | custom-call | tf_op jit(solution)/shard_map/finish/pallas_call | solution.py:514
  303.0 3.1 %copy.19 = bf16[1,65,64,64]{1,3,2,0:T(8,128)(2,1)} copy(bf16[1,65,64,64]{3,2,1,0:T(8,128)(2,1)} %bitcast.30) | data formatting | bytes 1064960
  (8 shorter events, 0.1 us)

commit v4 on v3

--- a/solution.py
+++ b/solution.py
@@ -27,8 +27,11 @@
 W_BLK = 512
 W_ROWS = 1792
 W_BUFS = 4
-KV_ROWS = 896
+KV_ROWS = 512
 H_BLK = 8
+CORE_HEADS = HEADS // 2
+HALF = CORE_HEADS * CHUNK
+RING = 3
 LAST_DIMS = (((1,), (1,)), ((), ()))
 BF16 = jnp.bfloat16
 F32 = jnp.float32
@@ -55,17 +58,19 @@
     return values * cos2 + swapped * sin2
 
 
-def layer_kernel(n, ids_ref, x_ref, bias_ref, rot_ref, gain_ref, cache_c, cache_kr, w_q, w_dkv, w_uk, w_uv,
+def layer_kernel(n, ids_ref, bias_ref, rot_ref, gain_ref, x_ref, cache_c, cache_kr, w_q, w_dkv, w_uk, w_uv,
                  o_lat, wuv_out, page_c_out, page_k_out,
-                 ids_in, ids_smem, cc, ck, kp, stage_c, stage_k, land_c, land_k, wbuf, q_all, qc, qk, m_ref, l_ref, acc,
-                 hbuf, h32, hout, kvbuf, new_c, new_k, kk, part_out, part_mid, part_fwd, part_in, c32,
-                 loc_sem, id_send, id_recv, c_send, c_recv, k_send, k_recv, p_send, p_recv, f_send, f_recv, w_sem, h_sem, ho_sem, kv_sem, out_sem):
+                 ids_in, ids_smem, cc, ck, kp, stage_c, stage_k, land_c, land_k, ring_c, ring_k, wbuf, q_all, qc, qk, m_ref, l_ref, acc,
+                 hbuf, h32, hout, kvbuf, xb, bias_p, rot_p, new_c, new_k, kk, part_out, part_mid, part_fwd, part_in, c32,
+                 loc_sem, id_send, id_recv, c_send, c_recv, k_send, k_recv, p_send, p_recv, f_send, f_recv, w_sem, h_sem, ho_sem, kv_sem, out_sem,
+                 pair_send, pair_recv, rc_send, rc_recv, rk_send, rk_recv, credit):
     me = lax.axis_index("pool")
     bits = n.bit_length() - 1
     pages = kp.shape[0]
-    n_blk = w_q.shape[1] // W_BLK
+    core = lax.rem(me, 2)
+    n_blk = w_q.shape[1] // 2 // W_BLK
     n_kv = D_MODEL // KV_ROWS
-    n_h = HEADS // H_BLK
+    n_h = CORE_HEADS // H_BLK
 
     load_c = pltpu.make_async_copy(cache_c.at[pl.ds(0, pages)], cc, loc_sem.at[0])
     load_k = pltpu.make_async_copy(cache_kr.at[pl.ds(0, pages)], ck, loc_sem.at[1])
@@ -74,6 +79,7 @@
 
     flips = flip_weights(me, bits)
     any_peer = lax.rem(me + 1, n)
+    partner = me + flips[0]
 
     def peer_of(k):
         return flipped(me, flips, step_code(k))
@@ -91,11 +97,19 @@
 
     def w_copy(col, r):
         rows = pl.ds(r * W_ROWS, W_ROWS)
-        return pltpu.make_async_copy(w_q.at[rows, pl.ds(pl.multiple_of(col * W_BLK, W_BLK), W_BLK)], wbuf.at[r], w_sem.at[r])
+        return pltpu.make_async_copy(w_q.at[rows, pl.ds(pl.multiple_of((core * n_blk + col) * W_BLK, W_BLK), W_BLK)], wbuf.at[r], w_sem.at[r])
 
     kv_copy(0, 0).start()
     kv_copy(1, 1).start()
+    own_x = pltpu.make_async_copy(x_ref, xb.at[pl.ds(0, CHUNK)], loc_sem.at[4])
+    own_x.start()
     pl.semaphore_wait(barrier, n - 1)
+
+    def pair_copy(i, src, dst):
+        return pltpu.make_async_remote_copy(src_ref=src, dst_ref=dst, send_sem=pair_send.at[i], recv_sem=pair_recv.at[i],
+                                            device_id=(partner,), device_id_type=MESH)
+
+    pair = [pair_copy(0, x_ref, xb.at[pl.ds(CHUNK, CHUNK)]), pair_copy(1, rot_ref, rot_p), pair_copy(2, bias_ref, bias_p)]
 
     def id_copy(k, peer):
         return pltpu.make_async_remote_copy(src_ref=ids_ref.at[peer], dst_ref=ids_in.at[k], send_sem=id_send.at[k],
@@ -107,6 +121,8 @@
 
     own_ids = pltpu.make_async_copy(ids_ref.at[me], ids_in.at[0], loc_sem.at[2])
     own_ids.start()
+    for c in pair:
+        c.start()
     load_k.wait()
 
     @pl.loop(0, pages)
@@ -133,40 +149,51 @@
         return pltpu.make_async_remote_copy(src_ref=stage_k.at[k], dst_ref=land_k.at[k], send_sem=k_send.at[k],
                                             recv_sem=k_recv.at[k], device_id=(peer,), device_id_type=MESH)
 
-    def send_pages(k):
+    def launch(k):
         peer = peer_of(k)
+        c_copy(k, peer).start()
+        k_copy(k, peer).start()
+
+    def send_pages(k, first):
         for s in range(SLOTS):
             page = ids_smem[k, 0, s]
             stage_c[k, s] = cc[page]
             stage_k[k, s] = kp[page]
-        c_copy(k, peer).start()
-        k_copy(k, peer).start()
+
+        @pl.when(k > first)
+        def _():
+            launch(k - 1)
 
     @pl.loop(1, n // 2)
     def _(k):
-        send_pages(k)
+        send_pages(k, 1)
+
+    launch(n // 2 - 1)
 
     for r in range(n_row):
         w_copy(0, r).start()
 
-    kv = jnp.zeros((CHUNK, LATENT + ROPE_DIM), F32)
+    own_x.wait()
+    for c in pair:
+        c.wait_recv()
+    kv = jnp.zeros((2 * CHUNK, LATENT + ROPE_DIM), F32)
     for i in range(n_kv):
         kv_copy(i, i % 2).wait()
-        kv = kv + lax.dot_general(x_ref[:, i * KV_ROWS:(i + 1) * KV_ROWS], kvbuf[i % 2], LAST_DIMS, preferred_element_type=F32)
+        kv = kv + lax.dot_general(xb[:, i * KV_ROWS:(i + 1) * KV_ROWS], kvbuf[i % 2], LAST_DIMS, preferred_element_type=F32)
         if i + 2 < n_kv:
             kv_copy(i + 2, i % 2).start()
     lat = kv[:, :LATENT]
     inv_rms = lax.rsqrt(jnp.mean(lat * lat, axis=-1, keepdims=True) + NORM_EPS)
     c_new = (lat * inv_rms * gain_ref[...]).astype(BF16)
-    cos2 = rot_ref[0]
-    sin2 = rot_ref[1]
+    cos2 = jnp.concatenate([rot_ref[0], rot_p[0]], axis=0)
+    sin2 = jnp.concatenate([rot_ref[1], rot_p[1]], axis=0)
     kr_new = rope(kv[:, LATENT:], cos2, sin2).astype(BF16)
     new_c[...] = c_new
     new_k[...] = kr_new
 
     for g in range(LATENT // 128):
-        c32[:, g, :] = c_new[:, g * 128:(g + 1) * 128].astype(F32)
-    c32[:, 4, :] = jnp.concatenate([kr_new, kr_new], axis=-1).astype(F32)
+        c32[:, g, :] = c_new[:CHUNK, g * 128:(g + 1) * 128].astype(F32)
+    c32[:, 4, :] = jnp.concatenate([kr_new[:CHUNK], kr_new[:CHUNK]], axis=-1).astype(F32)
     low = lax.broadcasted_iota(jnp.int32, (1, 128), 1) < ROPE_DIM
     for i in range(n):
         a = c32[2 * i]
@@ -190,19 +217,20 @@
 
     @pl.loop(n // 2, n)
     def _(k):
-        send_pages(k)
+        send_pages(k, n // 2)
 
     for s in range(SLOTS):
         page = ids_smem[0, 0, s]
         land_c[0, s] = cc[page]
         land_k[0, s] = kp[page]
+    launch(n - 1)
 
     @pl.loop(0, n_blk)
     def _(col):
-        total = jnp.zeros((CHUNK, W_BLK), F32)
+        total = jnp.zeros((2 * CHUNK, W_BLK), F32)
         for r in range(n_row):
             w_copy(col, r).wait()
-            total = total + jnp.dot(x_ref[:, r * W_ROWS:(r + 1) * W_ROWS], wbuf[r], preferred_element_type=F32)
+            total = total + jnp.dot(xb[:, r * W_ROWS:(r + 1) * W_ROWS], wbuf[r], preferred_element_type=F32)
 
             @pl.when(col + 1 < n_blk)
             def _():
@@ -211,7 +239,7 @@
         q_all[:, pl.ds(pl.multiple_of(col * W_BLK, W_BLK), W_BLK)] = total.astype(BF16)
 
     def h_copy(src, i, slot):
-        return pltpu.make_async_copy(src.at[:, pl.ds(pl.multiple_of(i * H_BLK, H_BLK), H_BLK)], hbuf.at[slot], h_sem.at[slot])
+        return pltpu.make_async_copy(src.at[:, pl.ds(pl.multiple_of(core * CORE_HEADS + i * H_BLK, H_BLK), H_BLK)], hbuf.at[slot], h_sem.at[slot])
 
     h_copy(w_uk, 0, 0).start()
 
@@ -235,8 +263,12 @@
                 u = lax.dot_general(q2[:, base:base + NOPE_DIM], wk, LAST_DIMS, preferred_element_type=F32)
                 qr = rope(q32[:, base + NOPE_DIM:base + NOPE_DIM + ROPE_DIM], cos2, sin2).astype(BF16)
                 at = pl.ds(pl.multiple_of((i * H_BLK + j) * CHUNK, CHUNK), CHUNK)
-                qc[at, :] = u.astype(BF16)
-                qk[at, :] = jnp.concatenate([qr, qr], axis=-1)
+                far = pl.ds(pl.multiple_of((CORE_HEADS + i * H_BLK + j) * CHUNK, CHUNK), CHUNK)
+                qc[at, :] = u[:CHUNK].astype(BF16)
+                qc[far, :] = u[CHUNK:].astype(BF16)
+                twice = jnp.concatenate([qr, qr], axis=-1)
+                qk[at, :] = twice[:CHUNK]
+                qk[far, :] = twice[CHUNK:]
 
     def ho_copy(i):
         return pltpu.make_async_copy(hout, wuv_out.at[pl.ds(pl.multiple_of(i * H_BLK, H_BLK), H_BLK)], ho_sem.at[0])
@@ -279,56 +311,95 @@
             lanes = slice(g * 128, (g + 1) * 128)
             acc[at, lanes] = acc[at, lanes] * alpha + pv[:, lanes]
 
-    first_lanes = lax.broadcasted_iota(jnp.int32, (CHUNK, 2 * ROPE_DIM), 1) < ROPE_DIM
-
-    @pl.loop(0, ROWS // (SUB * SUBS))
-    def _(i):
-        causal = (lax.broadcasted_iota(jnp.int32, (SUB, CHUNK), 1) <= lax.broadcasted_iota(jnp.int32, (SUB, CHUNK), 0) % CHUNK)
-        k64 = jnp.concatenate([new_k[...], jnp.zeros((CHUNK, ROPE_DIM), BF16)], axis=-1)
-        ats = [pl.ds(pl.multiple_of((i * SUBS + u) * SUB, SUB), SUB) for u in range(SUBS)]
-        raw = []
-        for at in ats:
-            s = lax.dot_general(qc[at, :], new_c[...], LAST_DIMS, preferred_element_type=F32)
-            raw.append(s + lax.dot_general(qk[at, :], k64, LAST_DIMS, preferred_element_type=F32))
-        for at, s in zip(ats, raw):
-            s = jnp.where(causal, s * SCALE2, -jnp.inf)
-            m = jnp.max(s, axis=-1, keepdims=True)
-            p = jnp.exp2(s - m)
-            m_ref[at, :] = jnp.broadcast_to(m, (SUB, 128))
-            l_ref[at, :] = jnp.concatenate([p, jnp.zeros((SUB, 128 - CHUNK), F32)], axis=-1)
-            acc[at, :] = jnp.dot(p.astype(BF16), new_c[...], preferred_element_type=F32)
+    def row_tiles(half, i):
+        return [pl.ds(pl.multiple_of(half * HALF + (i * SUBS + u) * SUB, SUB), SUB) for u in range(SUBS)]
+
+    for half in range(2):
+        @pl.loop(0, HALF // (SUB * SUBS))
+        def _(i):
+            causal = (lax.broadcasted_iota(jnp.int32, (SUB, CHUNK), 1) <= lax.broadcasted_iota(jnp.int32, (SUB, CHUNK), 0) % CHUNK)
+            c64 = new_c[half * CHUNK:(half + 1) * CHUNK, :]
+            k64 = jnp.concatenate([new_k[half * CHUNK:(half + 1) * CHUNK, :], jnp.zeros((CHUNK, ROPE_DIM), BF16)], axis=-1)
+            ats = row_tiles(half, i)
+            raw = []
+            for at in ats:
+                s = lax.dot_general(qc[at, :], c64, LAST_DIMS, preferred_element_type=F32)
+                raw.append(s + lax.dot_general(qk[at, :], k64, LAST_DIMS, preferred_element_type=F32))
+            for at, s in zip(ats, raw):
+                s = jnp.where(causal, s * SCALE2, -jnp.inf)
+                m = jnp.max(s, axis=-1, keepdims=True)
+                p = jnp.exp2(s - m)
+                m_ref[at, :] = jnp.broadcast_to(m, (SUB, 128))
+                l_ref[at, :] = jnp.concatenate([p, jnp.zeros((SUB, 128 - CHUNK), F32)], axis=-1)
+                acc[at, :] = jnp.dot(p.astype(BF16), c64, preferred_element_type=F32)
 
     half_low = lax.broadcasted_iota(jnp.int32, (PAGE_LEN // 2, 2 * ROPE_DIM), 1) < ROPE_DIM
 
-    @pl.loop(0, n // 2)
-    def _(t):
-        @pl.when(t > 0)
-        def _():
-            c_copy(2 * t, any_peer).wait_recv()
-            k_copy(2 * t, any_peer).wait_recv()
-
-        c_copy(2 * t + 1, any_peer).wait_recv()
-        k_copy(2 * t + 1, any_peer).wait_recv()
-
+    def spread(page_of):
         for d in range(2):
             for s in range(SLOTS):
-                page = land_k[2 * t + d, s]
+                page = page_of(d, s)
                 zero = jnp.zeros_like(page)
                 base = (d * SLOTS + s) * PAGE_LEN
                 kk[base:base + PAGE_LEN // 2, :] = jnp.where(half_low, page, zero)
                 kk[base + PAGE_LEN // 2:base + PAGE_LEN, :] = jnp.where(half_low, zero, page)
 
-        @pl.loop(0, ROWS // (SUB * SUBS))
+    def attend(half, keys_of, bias_of):
+        @pl.loop(0, HALF // (SUB * SUBS))
         def _(i):
-            keys = land_c[pl.ds(2 * t, 2)].reshape(2 * SLOTS * PAGE_LEN, LATENT)
-            bias = bias_ref[t]
-            ats = [pl.ds(pl.multiple_of((i * SUBS + u) * SUB, SUB), SUB) for u in range(SUBS)]
+            keys = keys_of().reshape(2 * SLOTS * PAGE_LEN, LATENT)
+            bias = bias_of()
+            ats = row_tiles(half, i)
             raw = []
             for at in ats:
                 s = lax.dot_general(qc[at, :], keys, LAST_DIMS, preferred_element_type=F32)
                 raw.append(s + lax.dot_general(qk[at, :], kk[...], LAST_DIMS, preferred_element_type=F32))
             for at, s in zip(ats, raw):
                 tile(at, s * SCALE2 + bias, keys)
+
+    steps = n // 2
+
+    def ring_copies(t):
+        r = lax.rem(t, RING)
+        return (pltpu.make_async_remote_copy(src_ref=land_c.at[pl.ds(2 * t, 2)], dst_ref=ring_c.at[r], send_sem=rc_send.at[r],
+                                             recv_sem=rc_recv.at[r], device_id=(partner,), device_id_type=MESH),
+                pltpu.make_async_remote_copy(src_ref=land_k.at[pl.ds(2 * t, 2)], dst_ref=ring_k.at[r], send_sem=rk_send.at[r],
+                                             recv_sem=rk_recv.at[r], device_id=(partner,), device_id_type=MESH))
+
+    @pl.loop(0, steps + 1)
+    def _(t):
+        @pl.when(t < steps)
+        def _():
+            @pl.when(t > 0)
+            def _():
+                c_copy(2 * t, any_peer).wait_recv()
+                k_copy(2 * t, any_peer).wait_recv()
+
+            c_copy(2 * t + 1, any_peer).wait_recv()
+            k_copy(2 * t + 1, any_peer).wait_recv()
+
+            @pl.when(t >= RING)
+            def _():
+                for c in ring_copies(t - RING):
+                    c.wait_send()
+                pl.semaphore_wait(credit, 1)
+
+            for c in ring_copies(t):
+                c.start()
+            spread(lambda d, s: land_k[2 * t + d, s])
+            attend(0, lambda: land_c[pl.ds(2 * t, 2)], lambda: bias_ref[t])
+
+        @pl.when(t > 0)
+        def _():
+            r = lax.rem(t - 1, RING)
+            for c in ring_copies(t - 1):
+                c.wait_recv()
+            spread(lambda d, s: ring_k[r, d, s])
+            attend(1, lambda: ring_c[r], lambda: bias_p[t - 1])
+
+            @pl.when(t - 1 < steps - RING)
+            def _():
+                pl.semaphore_signal(credit, inc=1, device_id=(partner,), device_id_type=MESH)
 
         @pl.when(t == n // 2 - 6)
         def _():
@@ -370,10 +441,10 @@
         c32[2 * i, 4:5] = part[8:9]
         c32[2 * i + 1, 4:5] = jnp.concatenate([part[8:9, ROPE_DIM:], part[8:9, :ROPE_DIM]], axis=-1)
     for g in range(LATENT // 128):
-        new_c[:, g * 128:(g + 1) * 128] = c32[:, g, :].astype(BF16)
-    new_k[...] = c32[:, 4, :][:, :ROPE_DIM].astype(BF16)
-    out_pc = pltpu.make_async_copy(new_c, page_c_out, out_sem.at[1])
-    out_pk = pltpu.make_async_copy(new_k, page_k_out, out_sem.at[2])
+        new_c[:CHUNK, g * 128:(g + 1) * 128] = c32[:, g, :].astype(BF16)
+    new_k[:CHUNK, :] = c32[:, 4, :][:, :ROPE_DIM].astype(BF16)
+    out_pc = pltpu.make_async_copy(new_c.at[pl.ds(0, CHUNK)], page_c_out, out_sem.at[1])
+    out_pk = pltpu.make_async_copy(new_k.at[pl.ds(0, CHUNK)], page_k_out, out_sem.at[2])
     out_pc.start()
     out_pk.start()
 
@@ -385,13 +456,18 @@
         p_copy(k, any_peer).wait_send()
         f_copy(k, any_peer).wait_send()
 
+    for c in pair:
+        c.wait_send()
+    for t in range(steps - RING, steps):
+        for c in ring_copies(t):
+            c.wait_send()
     ho_copy(n_h - 1).wait()
     out.wait()
     out_pc.wait()
     out_pk.wait()
 
 
-def layer(n, ids, x, bias, rot, gain, cache_c, cache_kr, w_q, w_dkv, w_uk, w_uv):
+def layer(n, ids, bias, rot, gain, x, cache_c, cache_kr, w_q, w_dkv, w_uk, w_uv):
     pages = cache_c.shape[0] - 1
     any_spec = pl.BlockSpec(memory_space=pl.ANY)
     vmem = pl.BlockSpec(memory_space=pltpu.VMEM)
@@ -401,11 +477,11 @@
         name="layer",
         out_shape=(
             jax.ShapeDtypeStruct((ROWS, LATENT), BF16),
-            jax.ShapeDtypeStruct((HEADS, LATENT, VALUE_DIM), BF16),
+            jax.ShapeDtypeStruct((CORE_HEADS, LATENT, VALUE_DIM), BF16),
             jax.ShapeDtypeStruct((CHUNK, LATENT), BF16),
             jax.ShapeDtypeStruct((CHUNK, ROPE_DIM), BF16),
         ),
-        in_specs=[vmem] * 5 + [any_spec] * 6,
+        in_specs=[vmem] * 4 + [any_spec] * 7,
         out_specs=(any_spec,) * 4,
         scratch_shapes=[
             pltpu.VMEM((n, 1, 128), jnp.int32),
@@ -417,8 +493,10 @@
             pltpu.VMEM((n, SLOTS, PAGE_LEN // 2, 2 * ROPE_DIM), BF16),
             pltpu.VMEM((n, SLOTS, PAGE_LEN, LATENT), BF16),
             pltpu.VMEM((n, SLOTS, PAGE_LEN // 2, 2 * ROPE_DIM), BF16),
+            pltpu.VMEM((RING, 2, SLOTS, PAGE_LEN, LATENT), BF16),
+            pltpu.VMEM((RING, 2, SLOTS, PAGE_LEN // 2, 2 * ROPE_DIM), BF16),
             pltpu.VMEM((W_BUFS, W_ROWS, W_BLK), BF16),
-            pltpu.VMEM((CHUNK, HEADS * (NOPE_DIM + ROPE_DIM)), BF16),
+            pltpu.VMEM((2 * CHUNK, CORE_HEADS * (NOPE_DIM + ROPE_DIM)), BF16),
             pltpu.VMEM((ROWS, LATENT), BF16),
             pltpu.VMEM((ROWS, 2 * ROPE_DIM), BF16),
             pltpu.VMEM((ROWS, 128), F32),
@@ -428,114 +506,174 @@
             pltpu.VMEM((LATENT, H_BLK, NOPE_DIM), F32),
             pltpu.VMEM((H_BLK, LATENT, VALUE_DIM), BF16),
             pltpu.VMEM((2, LATENT + ROPE_DIM, KV_ROWS), BF16),
-            pltpu.VMEM((CHUNK, LATENT), BF16),
-            pltpu.VMEM((CHUNK, ROPE_DIM), BF16),
+            pltpu.VMEM((2 * CHUNK, D_MODEL), BF16),
+            pltpu.VMEM(bias.shape, F32),
+            pltpu.VMEM(rot.shape, F32),
+            pltpu.VMEM((2 * CHUNK, LATENT), BF16),
+            pltpu.VMEM((2 * CHUNK, ROPE_DIM), BF16),
             pltpu.VMEM((2 * SLOTS * PAGE_LEN, 2 * ROPE_DIM), BF16),
             pltpu.VMEM((n, 16, 128), BF16),
             pltpu.VMEM((n, 16, 128), BF16),
             pltpu.VMEM((n, 16, 128), BF16),
             pltpu.VMEM((n, 16, 128), BF16),
             pltpu.VMEM((CHUNK, 8, 128), F32),
-            dma((4,)),
-        ] + [dma((n,))] * 10 + [dma((W_BUFS,)), dma((2,)), dma((1,)), dma((2,)), dma((3,))],
+            dma((5,)),
+        ] + [dma((n,))] * 10 + [dma((W_BUFS,)), dma((2,)), dma((1,)), dma((2,)), dma((3,)), dma((3,)), dma((3,))] + [dma((RING,))] * 4 + [pltpu.SemaphoreType.REGULAR],
         compiler_params=pltpu.CompilerParams(collective_id=0, has_side_effects=True, vmem_limit_bytes=VMEM_LIMIT),
-    )(ids, x, bias, rot, gain, cache_c, cache_kr, w_q, w_dkv, w_uk, w_uv)
-
-
-O_BLK = 256
-O_BUFS = 6
-
-
-def finish_kernel(x_ref, o_lat, wuv, w_o, cache_c, cache_kr, page_c, page_k, y_ref, out_c, out_kr,
-                  lat, wv, heads, wbuf, cbuf, kbuf, lat_sem, wv_sem, w_sem, in_sem, out_sem):
+    )(ids, bias, rot, gain, x, cache_c, cache_kr, w_q, w_dkv, w_uk, w_uv)
+
+
+O_BLK = 512
+O_BUFS = 7
+
+
+def finish_kernel(x_ref, o_lat, wuv, w_o, y_ref, lat, wv, heads, wbuf, own, going, coming, lat_sem, wv_sem, w_sem, s_send, s_recv):
+    me = lax.axis_index("pool")
+    core = lax.rem(me, 2)
+    partner = me + 1 - 2 * core
+    depth = CORE_HEADS * VALUE_DIM
     n_blk = w_o.shape[1] // O_BLK
-    n_h = HEADS // H_BLK
-    pages = cache_c.shape[0] - 1
-
-    def lat_copy(i):
-        at = pl.ds(pl.multiple_of(i * H_BLK * CHUNK, 8), H_BLK * CHUNK)
-        return pltpu.make_async_copy(o_lat.at[at], lat.at[at], lat_sem.at[i])
+    n_h = CORE_HEADS // H_BLK
+
+    def lat_copy(half, i):
+        at = pl.ds(pl.multiple_of(half * HALF + i * H_BLK * CHUNK, 8), H_BLK * CHUNK)
+        return pltpu.make_async_copy(o_lat.at[at], lat.at[at], lat_sem.at[half, i])
 
     def wv_copy(i):
         at = pl.ds(pl.multiple_of(i * H_BLK, H_BLK), H_BLK)
         return pltpu.make_async_copy(wuv.at[at], wv.at[at], wv_sem.at[i])
 
     def w_copy(i, slot):
-        return pltpu.make_async_copy(w_o.at[:, pl.ds(pl.multiple_of(i * O_BLK, O_BLK), O_BLK)], wbuf.at[slot], w_sem.at[slot])
+        rows = pl.ds(pl.multiple_of(core * depth, depth), depth)
+        return pltpu.make_async_copy(w_o.at[rows, pl.ds(pl.multiple_of(i * O_BLK, O_BLK), O_BLK)], wbuf.at[slot], w_sem.at[slot])
+
+    def send(i):
+        return pltpu.make_async_remote_copy(src_ref=going.at[i], dst_ref=coming.at[i], send_sem=s_send.at[i], recv_sem=s_recv.at[i],
+                                            device_id=(partner,), device_id_type=MESH)
 
     for i in range(n_h):
-        lat_copy(i).start()
+        for half in range(2):
+            lat_copy(half, i).start()
         wv_copy(i).start()
-    ins = [pltpu.make_async_copy(cache_c.at[pl.ds(0, pages)], cbuf.at[pl.ds(0, pages)], in_sem.at[0]),
-           pltpu.make_async_copy(cache_kr.at[pl.ds(0, pages)], kbuf.at[pl.ds(0, pages)], in_sem.at[1]),
-           pltpu.make_async_copy(page_c, cbuf.at[pages], in_sem.at[2]),
-           pltpu.make_async_copy(page_k, kbuf.at[pages], in_sem.at[3])]
     for i in range(O_BUFS):
         w_copy(i, i).start()
-    for c in ins:
-        c.start()
+
+    barrier = pltpu.get_barrier_semaphore()
+    pl.semaphore_signal(barrier, inc=1, device_id=(partner,), device_id_type=MESH)
+    pl.semaphore_wait(barrier, 1)
 
     @pl.loop(0, n_h)
     def _(i):
-        lat_copy(i).wait()
+        for half in range(2):
+            lat_copy(half, i).wait()
         wv_copy(i).wait()
         for j in range(H_BLK):
             h = i * H_BLK + j
-            o = jnp.dot(lat[pl.ds(pl.multiple_of(h * CHUNK, CHUNK), CHUNK), :], wv[h], preferred_element_type=F32)
+            near = lat[pl.ds(pl.multiple_of(h * CHUNK, CHUNK), CHUNK), :]
+            far = lat[pl.ds(pl.multiple_of(HALF + h * CHUNK, CHUNK), CHUNK), :]
+            o = jnp.dot(jnp.concatenate([near, far], axis=0), wv[h], preferred_element_type=F32)
             heads[:, pl.ds(pl.multiple_of(h * VALUE_DIM, VALUE_DIM), VALUE_DIM)] = o.astype(BF16)
-
-    for c in ins:
-        c.wait()
-    outs = [pltpu.make_async_copy(cbuf, out_c, out_sem.at[0]), pltpu.make_async_copy(kbuf, out_kr, out_sem.at[1])]
-    for c in outs:
-        c.start()
 
     @pl.loop(0, n_blk)
     def _(i):
         slot = lax.rem(i, O_BUFS)
         w_copy(i, slot).wait()
-        at = pl.ds(pl.multiple_of(i * O_BLK, O_BLK), O_BLK)
         part = jnp.dot(heads[...], wbuf[slot], preferred_element_type=F32)
-        y_ref[:, at] = (x_ref[:, at].astype(F32) + part).astype(BF16)
 
         @pl.when(i + O_BUFS < n_blk)
         def _():
             w_copy(i + O_BUFS, slot).start()
 
-    for c in outs:
-        c.wait()
-
-
-def finish(x, o_lat, wuv, w_o, cache_c, cache_kr, page_c, page_k):
+        own[i] = part[:CHUNK]
+        going[i] = part[CHUNK:]
+
+        @pl.when(i > 0)
+        def _():
+            send(i - 1).start()
+
+    for i in range(n_blk):
+        if i == 1:
+            send(n_blk - 1).start()
+        send(i).wait_recv()
+        at = slice(i * O_BLK, (i + 1) * O_BLK)
+        y_ref[:, at] = (x_ref[:, at].astype(F32) + (own[i] + coming[i])).astype(BF16)
+    for i in range(n_blk):
+        send(i).wait_send()
+
+
+def finish(x, o_lat, wuv, w_o):
     any_spec = pl.BlockSpec(memory_space=pl.ANY)
     vmem = pl.BlockSpec(memory_space=pltpu.VMEM)
     dma = pltpu.SemaphoreType.DMA
-    n_h = HEADS // H_BLK
+    n_h = CORE_HEADS // H_BLK
+    n_blk = w_o.shape[1] // O_BLK
     return pl.pallas_call(
         finish_kernel,
         name="finish",
-        out_shape=(
-            jax.ShapeDtypeStruct(x.shape, BF16),
-            jax.ShapeDtypeStruct(cache_c.shape, BF16),
-            jax.ShapeDtypeStruct(cache_kr.shape, BF16),
-        ),
-        in_specs=[vmem] + [any_spec] * 7,
-        out_specs=(vmem, any_spec, any_spec),
+        out_shape=jax.ShapeDtypeStruct(x.shape, BF16),
+        in_specs=[vmem] + [any_spec] * 3,
+        out_specs=vmem,
         scratch_shapes=[
             pltpu.VMEM(o_lat.shape, BF16),
             pltpu.VMEM(wuv.shape, BF16),
-            pltpu.VMEM((CHUNK, HEADS * VALUE_DIM), BF16),
-            pltpu.VMEM((O_BUFS, HEADS * VALUE_DIM, O_BLK), BF16),
+            pltpu.VMEM((2 * CHUNK, CORE_HEADS * VALUE_DIM), BF16),
+            pltpu.VMEM((O_BUFS, CORE_HEADS * VALUE_DIM, O_BLK), BF16),
+            pltpu.VMEM((n_blk, CHUNK, O_BLK), F32),
+            pltpu.VMEM((n_blk, CHUNK, O_BLK), F32),
+            pltpu.VMEM((n_blk, CHUNK, O_BLK), F32),
+            dma((2, n_h)),
+            dma((n_h,)),
+            dma((O_BUFS,)),
+            dma((n_blk,)),
+            dma((n_blk,)),
+        ],
+        compiler_params=pltpu.CompilerParams(collective_id=1, has_side_effects=True, vmem_limit_bytes=VMEM_LIMIT),
+    )(x, o_lat, wuv, w_o)
+
+
+COPY_PARTS = 8
+
+
+def cache_kernel(cache_c, cache_kr, page_c, page_k, out_c, out_kr, cbuf, kbuf, in_sem, out_sem):
+    pages = cache_c.shape[0] - 1
+    step = pages // COPY_PARTS
+    ins, outs = [], []
+    for i in range(COPY_PARTS):
+        at = pl.ds(i * step, step)
+        ins.append(pltpu.make_async_copy(cache_c.at[at], cbuf.at[at], in_sem.at[i]))
+        outs.append(pltpu.make_async_copy(cbuf.at[at], out_c.at[at], out_sem.at[i]))
+    at = pl.ds(0, pages)
+    last = pl.ds(pages, 1)
+    ins += [pltpu.make_async_copy(cache_kr.at[at], kbuf.at[at], in_sem.at[COPY_PARTS]),
+            pltpu.make_async_copy(page_c, cbuf.at[pages], in_sem.at[COPY_PARTS + 1]),
+            pltpu.make_async_copy(page_k, kbuf.at[pages], in_sem.at[COPY_PARTS + 2])]
+    outs += [pltpu.make_async_copy(kbuf.at[at], out_kr.at[at], out_sem.at[COPY_PARTS]),
+             pltpu.make_async_copy(cbuf.at[last], out_c.at[last], out_sem.at[COPY_PARTS + 1]),
+             pltpu.make_async_copy(kbuf.at[last], out_kr.at[last], out_sem.at[COPY_PARTS + 2])]
+    for c in ins:
+        c.start()
+    for c, o in zip(ins, outs):
+        c.wait()
+        o.start()
+    for o in outs:
+        o.wait()
+
+
+def update_cache(cache_c, cache_kr, page_c, page_k):
+    any_spec = pl.BlockSpec(memory_space=pl.ANY)
+    return pl.pallas_call(
+        cache_kernel,
+        name="cache",
+        out_shape=(jax.ShapeDtypeStruct(cache_c.shape, BF16), jax.ShapeDtypeStruct(cache_kr.shape, BF16)),
+        in_specs=[any_spec] * 4,
+        out_specs=(any_spec, any_spec),
+        scratch_shapes=[
             pltpu.VMEM(cache_c.shape, BF16),
             pltpu.VMEM(cache_kr.shape, BF16),
-            dma((n_h,)),
-            dma((n_h,)),
-            dma((O_BUFS,)),
-            dma((4,)),
-            dma((2,)),
+            pltpu.SemaphoreType.DMA((COPY_PARTS + 3,)),
+            pltpu.SemaphoreType.DMA((COPY_PARTS + 3,)),
         ],
-        compiler_params=pltpu.CompilerParams(vmem_limit_bytes=VMEM_LIMIT),
-    )(x, o_lat, wuv, w_o, cache_c, cache_kr, page_c, page_k)
+    )(cache_c, cache_kr, page_c, page_k)
 
 
 def solution(mesh):
@@ -560,8 +698,9 @@
         bias = jnp.where((keys // PAGE_LEN) % SLOTS < counts, 0.0, -jnp.inf).astype(F32)[:, None, :]
         cos_tab, sin_tab = rope_tables(pre_len[0] + jnp.arange(CHUNK))
         rot = jnp.stack([jnp.concatenate([cos_tab, cos_tab], -1), jnp.concatenate([-sin_tab, sin_tab], -1)])
-        o_lat, wuv, page_c, page_k = layer(n, ids, x, bias, rot, g_kv.astype(F32)[None], cache_c[0], cache_kr[0], w_q, w_dkv.T, w_uk, w_uv)
-        y, out_c, out_kr = finish(x, o_lat, wuv, w_o, cache_c[0], cache_kr[0], page_c, page_k)
+        o_lat, wuv, page_c, page_k = layer(n, ids, bias, rot, g_kv.astype(F32)[None], x, cache_c[0], cache_kr[0], w_q, w_dkv.T, w_uk, w_uv)
+        y = finish(x, o_lat, wuv, w_o)
+        out_c, out_kr = update_cache(cache_c[0], cache_kr[0], page_c, page_k)
         return y[None], out_c[None], out_kr[None]
 
     row_spec = P("pool")

time: 307 us -> 300 us (0.977)
  the two profiles are of different devices: /device:TPU:8 before, /device:TPU:17 now
where the time goes in v4:
time: 300 us
  Pallas kernels  284 us (95%)
  local copies, waits for them, and re-layouts  8.55 us (3%)
  other arithmetic  5.57 us (2%)
    pallas_call x1, Pallas kernels, layer(): pl.pallas_call(functools.partial(layer_kernel, n), name='layer', out_shap...  252 us
    pallas_call x1, Pallas kernels, finish(): pl.pallas_call(finish_kernel, name='finish', out_shape=jax.ShapeDtypeStru...  27.1 us
    unnamed x5, local copies, waits for them, and re-layouts  7.54 us

profile of v4, /device:TPU:17, one launch (start us, length us, event | category | flops | bytes accessed | tf_op | source)
XLA Modules:
  0.0 299.5 jit_solution(4330998614358716903)
XLA Ops:
  1.3 0.8 slice_bitcast_fusion.1
  2.1 0.2 select_reduce_fusion.1
  2.3 0.7 compare_select_fusion.1
  3.0 1.3 broadcast_in_dim.102
  4.2 0.1 add_select_fusion
  4.3 0.2 select_reduce_fusion
  4.5 1.3 broadcast_select_fusion.ids_ref
  5.8 0.2 multiply_cosine_fusion
  6.0 0.1 maximum_bitcast_fusion
  6.1 0.6 pad_maximum_fusion.rot_ref
  6.7 0.1 add_xor_fusion
  6.9 0.2 select_reduce_fusion.2
  7.1 0.1 copy.17
  7.1 0.1 broadcast_in_dim.94
  7.2 0.1 reshape.162
  7.3 0.6 compare_select_fusion.bias_ref
  7.9 3.6 %copy.18 = bf16[1,65,64,64]{3,2,1,0:T(8,128)(2,1)} copy(bf16[1,65,64,64]{1,3,2,0:T(8,128)(2,1)} %param.17) | data formatting | bytes 1064960 | tf_op args[5]
  11.5 251.9 %layer.1 = (bf16[4096,512]{1,0:T(8,128)(2,1)}, bf16[32,512,128]{2,1,0:T(8,128)(2,1)}, bf16[64,512]{1,0:T(8,128)(2,1)}, bf16[64,64]{1,0:T(8,128)(2,1)}) custom-call(s32[32,1,128]{2,1,0:T(1,128)} %broadcast_select_fusion.ids_ref, f32[16,1,512]{2,1,0:T(1,128)} %compare_select_fusion.bias_ref, f32[2,64,64]{2,1,0:T(8,128)} %pad_maximum_fusion.rot_ref, ...), custom_call_target="tpu_custom_call" | custom-call | tf_op jit(solution)/shard_map/layer/pallas_call | solution.py:475
  263.4 27.1 %finish.1 = bf16[64,7168]{1,0:T(8,128)(2,1)} custom-call(bf16[64,7168]{1,0:T(8,128)(2,1)} %bitcast.30, bf16[4096,512]{1,0:T(8,128)(2,1)} %get-tuple-element.9.o_lat, bf16[32,512,128]{2,1,0:T(8,128)(2,1)} %get-tuple-element.10.wuv, bf16[8192,7168]{1,0:T(8,128)(2,1)} %w_o.1), custom_call_target="tpu_custom_call" | custom-call | tf_op jit(solution)/shard_map/finish/pallas_call | solution.py:610
  290.5 0.0 copy-start
  290.5 5.0 %cache.1 = (bf16[65,64,512]{2,1,0:T(8,128)(2,1)}, bf16[65,64,64]{2,1,0:T(8,128)(2,1)}) custom-call(bf16[65,64,512]{2,1,0:T(8,128)(2,1)} %bitcast.24, bf16[65,64,64]{2,1,0:T(8,128)(2,1)} %bitcast.26, bf16[64,512]{1,0:T(8,128)(2,1)} %get-tuple-element.11.page_c, bf16[64,64]{1,0:T(8,128)(2,1)} %get-tuple-element.12.page_k), custom_call_target="tpu_custom_call" | custom-call | tf_op jit(solution)/shard_map/cache/pallas_call | solution.py:664
  295.5 3.1 %copy.19 = bf16[1,65,64,64]{1,3,2,0:T(8,128)(2,1)} copy(bf16[1,65,64,64]{3,2,1,0:T(8,128)(2,1)} %bitcast.31) | data formatting | bytes 1064960
  298.6 0.0 copy-done
  298.6 0.9 copy.22
  (8 shorter events, 0.1 us)
Async XLA Ops:
  290.5 8.1 %copy-start = (bf16[64,7168]{1,0:T(8,128)(2,1)S(1)}, bf16[64,7168]{1,0:T(8,128)(2,1)}, u32[]{:S(2)}) copy-start(bf16[64,7168]{1,0:T(8,128)(2,1)} %finish.1) | copy-start | bytes 2752516

commit v5 on v4

--- a/solution.py
+++ b/solution.py
@@ -38,7 +38,8 @@
 
 
 def step_code(k):
-    return lax.div(k, 2) + 16 * lax.rem(k, 2)
+    i, q = lax.div(k, 4), lax.rem(k, 4)
+    return i + 8 * (2 * lax.rem(lax.div(q + 1, 2), 2) + lax.div(q, 2))
 
 
 def flip_weights(me, bits):
@@ -692,7 +693,8 @@
         asked = jnp.sum(jnp.where(pos[None, None, :] == slot_of[:, :, None], pre_table[0, :, 1], 0), axis=2)
         ids = jnp.where(lanes == SLOTS, wr_table[0, 0, 0], asked)[:, None, :].astype(jnp.int32)
         keys = jnp.arange(2 * SLOTS * PAGE_LEN, dtype=jnp.int32)
-        owner_of = jnp.bitwise_xor(me, jnp.arange(n // 2, dtype=jnp.int32)[:, None] + 16 * (keys // (SLOTS * PAGE_LEN)))
+        codes = step_code(2 * jnp.arange(n // 2, dtype=jnp.int32)[:, None] + keys // (SLOTS * PAGE_LEN))
+        owner_of = jnp.bitwise_xor(me, codes)
         counts = jnp.sum(jnp.where(owner_of[:, :: SLOTS * PAGE_LEN, None] == owners, 1, 0), axis=2)
         counts = jnp.repeat(counts, SLOTS * PAGE_LEN, axis=1)
         bias = jnp.where((keys // PAGE_LEN) % SLOTS < counts, 0.0, -jnp.inf).astype(F32)[:, None, :]

time: 300 us -> 295 us (0.983)
  the two profiles are of different devices: /device:TPU:17 before, /device:TPU:0 now
where the time goes in v5:
time: 295 us
  Pallas kernels  279 us (95%)
  local copies, waits for them, and re-layouts  8.55 us (3%)
  other arithmetic  5.81 us (2%)
    pallas_call x1, Pallas kernels, layer(): pl.pallas_call(functools.partial(layer_kernel, n), name='layer', out_shap...  248 us
    pallas_call x1, Pallas kernels, finish(): pl.pallas_call(finish_kernel, name='finish', out_shape=jax.ShapeDtypeStru...  25.7 us
    unnamed x5, local copies, waits for them, and re-layouts  7.54 us

profile of v5, /device:TPU:0, one launch (start us, length us, event | category | flops | bytes accessed | tf_op | source)
XLA Modules:
  0.0 294.8 jit_solution(4957394497726457595)
XLA Ops:
  1.4 0.8 slice_bitcast_fusion.1
  2.1 0.2 select_reduce_fusion.1
  2.3 0.7 compare_select_fusion.1
  3.0 1.3 broadcast_in_dim.102
  4.2 0.1 add_select_fusion.1
  4.3 0.2 select_reduce_fusion
  4.5 1.3 broadcast_select_fusion.ids_ref
  5.8 0.2 multiply_cosine_fusion
  6.0 0.1 maximum_bitcast_fusion
  6.1 0.6 pad_maximum_fusion.rot_ref
  6.7 0.4 fusion.1
  7.1 0.2 select_reduce_fusion.2
  7.3 0.1 copy.17
  7.4 0.1 broadcast_in_dim.94
  7.5 0.1 reshape.166
  7.5 0.6 compare_select_fusion.bias_ref
  8.2 3.6 %copy.18 = bf16[1,65,64,64]{3,2,1,0:T(8,128)(2,1)} copy(bf16[1,65,64,64]{1,3,2,0:T(8,128)(2,1)} %param.17) | data formatting | bytes 1064960 | tf_op args[5]
  11.7 248.3 %layer.1 = (bf16[4096,512]{1,0:T(8,128)(2,1)}, bf16[32,512,128]{2,1,0:T(8,128)(2,1)}, bf16[64,512]{1,0:T(8,128)(2,1)}, bf16[64,64]{1,0:T(8,128)(2,1)}) custom-call(s32[32,1,128]{2,1,0:T(1,128)} %broadcast_select_fusion.ids_ref, f32[16,1,512]{2,1,0:T(1,128)} %compare_select_fusion.bias_ref, f32[2,64,64]{2,1,0:T(8,128)} %pad_maximum_fusion.rot_ref, ...), custom_call_target="tpu_custom_call" | custom-call | tf_op jit(solution)/shard_map/layer/pallas_call | solution.py:476
  260.0 25.7 %finish.1 = bf16[64,7168]{1,0:T(8,128)(2,1)} custom-call(bf16[64,7168]{1,0:T(8,128)(2,1)} %bitcast.30, bf16[4096,512]{1,0:T(8,128)(2,1)} %get-tuple-element.9.o_lat, bf16[32,512,128]{2,1,0:T(8,128)(2,1)} %get-tuple-element.10.wuv, bf16[8192,7168]{1,0:T(8,128)(2,1)} %w_o.1), custom_call_target="tpu_custom_call" | custom-call | tf_op jit(solution)/shard_map/finish/pallas_call | solution.py:611
  285.7 0.0 copy-start
  285.7 5.0 %cache.1 = (bf16[65,64,512]{2,1,0:T(8,128)(2,1)}, bf16[65,64,64]{2,1,0:T(8,128)(2,1)}) custom-call(bf16[65,64,512]{2,1,0:T(8,128)(2,1)} %bitcast.24, bf16[65,64,64]{2,1,0:T(8,128)(2,1)} %bitcast.26, bf16[64,512]{1,0:T(8,128)(2,1)} %get-tuple-element.11.page_c, bf16[64,64]{1,0:T(8,128)(2,1)} %get-tuple-element.12.page_k), custom_call_target="tpu_custom_call" | custom-call | tf_op jit(solution)/shard_map/cache/pallas_call | solution.py:665
  290.8 3.1 %copy.19 = bf16[1,65,64,64]{1,3,2,0:T(8,128)(2,1)} copy(bf16[1,65,64,64]{3,2,1,0:T(8,128)(2,1)} %bitcast.31) | data formatting | bytes 1064960
  293.8 0.0 copy-done
  293.8 0.9 copy.22
  (9 shorter events, 0.1 us)
Async XLA Ops:
  285.7 8.1 %copy-start = (bf16[64,7168]{1,0:T(8,128)(2,1)S(1)}, bf16[64,7168]{1,0:T(8,128)(2,1)}, u32[]{:S(2)}) copy-start(bf16[64,7168]{1,0:T(8,128)(2,1)} %finish.1) | copy-start | bytes 2752516
